TPU v7x, 32 devices: a 4x4x1 block of a 4x4x8 slice. The times are simulated.
32 devices in a mesh: dp: 1 (over z), y: 4 (over y), x: 8 (over x, core).
Axes of the slice: x: 4, y: 4, z: 1, core: 2. Of those that a mesh axis runs over, the one named last changes fastest.
The devices are a block of a 4x4x8 slice.
Arguments:
- tokens: int32 [3, 256], P(None, 'dp')
- lengths: int32 [256], P('dp')
- choices: int32 [3, 256, 8], P(None, 'dp')
- emb_table: bfloat16 [50304, 2048], P(None, 'x')
- k_cache: bfloat16 [256, 128, 16, 128], P('dp', None, 'y')
- v_cache: bfloat16 [256, 128, 16, 128], P('dp', None, 'y')
- g_attn: bfloat16 [2048], P('x')
- w_q: bfloat16 [2048, 2048], P('x', 'y')
- w_k: bfloat16 [2048, 2048], P('x', 'y')
- w_v: bfloat16 [2048, 2048], P('x', 'y')
- w_o: bfloat16 [2048, 2048], P('y', 'x')
- g_ffn: bfloat16 [2048], P('x')
- w_router: bfloat16 [2048, 64], P('x')
- w_act: bfloat16 [64, 2048, 1024], P(None, 'x', 'y')
- w_lin: bfloat16 [64, 2048, 1024], P(None, 'x', 'y')
- w_down: bfloat16 [64, 1024, 2048], P(None, 'y', 'x')
Outputs:
- output 1: bfloat16 [3, 256, 2048], P(None, 'dp', 'x')
- output 2: bfloat16 [256, 128, 16, 128], P('dp', None, 'y')
- output 3: bfloat16 [256, 128, 16, 128], P('dp', None, 'y')
All inputs are finite; a program needn't handle non-finite values.
Results may differ from a plain program's by a relative error of at most 0.0126822.
Values are sent between devices in bfloat16 or wider.
A program may use at most 768 MiB of HBM per device.

v0:
```python
import jax
import jax.numpy as jnp
from jax import lax
from jax.sharding import PartitionSpec as P

EPS = 1e-5
ROPE_BASE = 1.0e6


def shard_norm(x_val, gain_vec, width_full):
    x_f32 = x_val.astype(jnp.float32)
    sq_total = lax.psum(jnp.sum(x_f32 * x_f32, axis=-1, keepdims=True), 'x')
    return (x_f32 * lax.rsqrt(sq_total / width_full + EPS) * gain_vec.astype(jnp.float32)).astype(jnp.bfloat16)


def rotate(vectors, positions):
    head_dim = vectors.shape[-1]
    half_dim = head_dim // 2
    inv_freq = ROPE_BASE ** (-(jnp.arange(half_dim, dtype=jnp.float32) * 2.0 / head_dim))
    angle_shape = (vectors.shape[0],) + (1,) * (vectors.ndim - 2) + (half_dim,)
    angles = (positions.astype(jnp.float32)[:, None] * inv_freq[None, :]).reshape(angle_shape)
    cosine = jnp.cos(angles)
    sine_val = jnp.sin(angles)
    first_half = vectors[..., :half_dim].astype(jnp.float32)
    second_half = vectors[..., half_dim:].astype(jnp.float32)
    return jnp.concatenate([first_half * cosine - second_half * sine_val, second_half * cosine + first_half * sine_val], axis=-1).astype(jnp.bfloat16)


def write_slot(cache_arr, new_rows, positions):
    hit_mask = (jnp.arange(cache_arr.shape[1])[None, :] == positions[:, None])[:, :, None, None]
    return jnp.where(hit_mask, new_rows[:, None], cache_arr)


def attention(queries, key_cache, val_cache, positions):
    head_dim = queries.shape[-1]
    scores = jnp.einsum('bkgh,bskh->bkgs', queries, key_cache, preferred_element_type=jnp.float32) * head_dim ** -0.5
    valid_mask = (jnp.arange(key_cache.shape[1])[None, :] <= positions[:, None])[:, None, None, :]
    scores = jnp.where(valid_mask, scores, -1.0e30)
    peak_val = jnp.max(scores, axis=-1, keepdims=True)
    weight = jnp.where(valid_mask, jnp.exp(scores - peak_val), 0.0)
    total_w = jnp.sum(weight, axis=-1, keepdims=True)
    mixed_out = jnp.einsum('bkgs,bskh->bkgh', weight.astype(jnp.bfloat16), val_cache, preferred_element_type=jnp.float32)
    return (mixed_out / total_w).astype(jnp.bfloat16)


def mixing(logits, choice_row, experts):
    gate_val = jax.nn.softmax(jnp.take_along_axis(logits, choice_row, axis=1), axis=-1)
    onehot = choice_row[:, :, None] == jnp.arange(experts)[None, None, :]
    return jnp.sum(jnp.where(onehot, gate_val[:, :, None], 0.0), axis=1)


def solution(mesh):
    x_count = mesh.shape['x']
    cache_spec = P('dp', None, 'y', None)
    in_specs = (P(None, 'dp'), P('dp'), P(None, 'dp', None), P(None, 'x'), cache_spec, cache_spec, P('x'), P('x', 'y'), P('x', 'y'), P('x', 'y'), P('y', 'x'), P('x'), P('x', None), P(None, 'x', 'y'), P(None, 'x', 'y'), P(None, 'y', 'x'))
    out_specs = (P(None, 'dp', 'x'), cache_spec, cache_spec)

    def per_device(tokens, lengths, choices, emb_table, k_cache, v_cache, g_attn, w_q, w_k, w_v, w_o, g_ffn, w_router, w_act, w_lin, w_down):
        n_batch = tokens.shape[1]
        kv_local, head_dim = k_cache.shape[2], k_cache.shape[3]
        q_cols = w_q.shape[1]
        kv_cols = w_k.shape[1]
        group_size = q_cols // head_dim // kv_local
        width_full = emb_table.shape[1] * x_count
        experts = w_act.shape[0]
        key_cache, val_cache = k_cache, v_cache
        step_outs = []
        for step_idx in range(tokens.shape[0]):
            positions = lengths + step_idx
            x_in = jnp.take(emb_table, tokens[step_idx], axis=0)
            normed = shard_norm(x_in, g_attn, width_full)
            proj_part = jnp.concatenate([jnp.dot(normed, w_q, preferred_element_type=jnp.float32), jnp.dot(normed, w_k, preferred_element_type=jnp.float32), jnp.dot(normed, w_v, preferred_element_type=jnp.float32)], axis=1).astype(jnp.bfloat16)
            proj_sum = lax.psum(proj_part, 'x')
            queries = rotate(proj_sum[:, :q_cols].reshape(n_batch, kv_local, group_size, head_dim), positions)
            new_keys = rotate(proj_sum[:, q_cols:q_cols + kv_cols].reshape(n_batch, kv_local, head_dim), positions)
            new_vals = proj_sum[:, q_cols + kv_cols:].reshape(n_batch, kv_local, head_dim)
            key_cache = write_slot(key_cache, new_keys, positions)
            val_cache = write_slot(val_cache, new_vals, positions)
            mixed = attention(queries, key_cache, val_cache, positions).reshape(n_batch, q_cols)
            attn_sum = lax.psum(jnp.dot(mixed, w_o, preferred_element_type=jnp.float32).astype(jnp.bfloat16), 'y')
            x_mid = (x_in.astype(jnp.float32) + attn_sum.astype(jnp.float32)).astype(jnp.bfloat16)
            normed2 = shard_norm(x_mid, g_ffn, width_full)
            logits = lax.psum(jnp.dot(normed2, w_router, preferred_element_type=jnp.float32), 'x')
            coef = mixing(logits, choices[step_idx], experts)
            hidden_part = jnp.stack([jnp.einsum('bd,edf->ebf', normed2, w_act, preferred_element_type=jnp.float32), jnp.einsum('bd,edf->ebf', normed2, w_lin, preferred_element_type=jnp.float32)]).astype(jnp.bfloat16)
            hidden_sum = lax.psum(hidden_part, 'x')
            unit_bf16 = (coef.T[:, :, None] * jax.nn.silu(hidden_sum[0].astype(jnp.float32)) * hidden_sum[1].astype(jnp.float32)).astype(jnp.bfloat16)
            moe_sum = lax.psum(jnp.einsum('ebf,efd->bd', unit_bf16, w_down, preferred_element_type=jnp.float32).astype(jnp.bfloat16), 'y')
            step_outs.append((x_mid.astype(jnp.float32) + moe_sum.astype(jnp.float32)).astype(jnp.bfloat16))
        return jnp.stack(step_outs), key_cache, val_cache

    return jax.shard_map(per_device, mesh=mesh, in_specs=in_specs, out_specs=out_specs, check_vma=False)
```

profile of v0, /device:TPU:97, one launch (start us, length us, event | category | flops | bytes accessed | tf_op | source)
XLA Modules:
  0.0 1138.3 jit_solution(1055311498799362456)
XLA Ops:
  7.3 0.8 fusion.209
  8.2 0.7 convert_element_type.257
  8.9 12.6 %gather_fusion = bf16[256,256]{1,0:T(8,128)(2,1)S(1)} fusion(bf16[50304,256]{1,0:T(8,128)(2,1)} %param.23, s32[1024]{0:T(1024)S(1)} %pad_clamp_fusion.2), kind=kCustom, calls=%fused_computation.clone | custom fusion | bytes 263168 | tf_op jit(solution)/shard_map/jit(_take)/gather | solution.py:70
  21.5 12.7 %gather_fusion.4 = bf16[256,256]{1,0:T(8,128)(2,1)S(1)} fusion(bf16[50304,256]{1,0:T(8,128)(2,1)} %param.23, s32[1024]{0:T(1024)S(1)} %pad_clamp_fusion), kind=kCustom, calls=%fused_computation.3.clone | custom fusion | bytes 263168 | tf_op jit(solution)/shard_map/jit(_take)/gather | solution.py:70
  34.1 12.7 %gather_fusion.2 = bf16[256,256]{1,0:T(8,128)(2,1)S(1)} fusion(bf16[50304,256]{1,0:T(8,128)(2,1)} %param.23, s32[1024]{0:T(1024)S(1)} %pad_clamp_fusion.1), kind=kCustom, calls=%fused_computation.2.clone | custom fusion | bytes 263168 | tf_op jit(solution)/shard_map/jit(_take)/gather | solution.py:70
  47.7 13.9 %all-reduce.1 = (f32[256,1]{0,1:T(1,128)S(1)}, f32[256,1]{0,1:T(1,128)S(1)}, f32[256,1]{0,1:T(1,128)S(1)}) all-reduce(f32[256,1]{0,1:T(1,128)S(1)} %bitcast.303, f32[256,1]{0,1:T(1,128)S(1)} %bitcast.305, f32[256,1]{0,1:T(1,128)S(1)} %bitcast.304), channel_id=1, replica_groups=mesh['dp'=1,'y'=4,'x'=8] {'x'}, use_global_device_ids=true, to_apply=%region_1.3 | all-reduce | flops 768 | bytes 6144 | tf_op jit(solution)/shard_map/psum | solution.py:12
  61.9 1.2 convolution_convert_fusion
  63.4 1.2 convolution_convert_fusion.3
  64.6 1.2 convolution_convert_fusion.2
  65.9 1.2 convolution_convert_fusion.5
  67.4 1.2 convolution_convert_fusion.6
  68.6 1.2 convolution_convert_fusion.8
  69.9 0.9 pad_maximum_fusion.5
  70.8 0.9 pad_maximum_fusion.4
  71.7 0.9 pad_maximum_fusion.3
  72.8 0.8 multiply_cosine_fusion.2
  74.2 0.7 iota_compare_fusion.8
  74.9 0.8 iota_compare_fusion.4
  75.7 59.1 %all-reduce.17.cloned.1.call-done = (bf16[256,1536]{1,0:T(8,128)(2,1)}, bf16[256,1536]{1,0:T(8,128)(2,1)}, bf16[256,1536]{1,0:T(8,128)(2,1)}) async-done(((bf16[256,1536]{1,0:T(8,128)(2,1)}, bf16[256,1536]{1,0:T(8,128)(2,1)}, bf16[256,1536]{1,0:T(8,128)(2,1)}), (bf16[256,1536]{1,0:T(8,128)(2,1)}, bf16[256,1536]{1,0:T(8,128)(2,1)}, bf16[256,1536]{1,0:T(8,128)(2,1)})) %all-reduce.17.cloned.1.call-update) | async-done | bytes 2359312 | tf_op jit(solution)/shard_map/psum | solution.py:73
  134.8 1.2 fusion.204
  136.3 1.2 fusion.203
  138.3 1.2 fusion.205
  140.9 124.7 %broadcast_select_fusion.1 = (bf16[256,128,4,128]{3,2,1,0:T(4,128)(2,1)}, bf16[256,128,4,128]{3,2,1,0:T(4,128)(2,1)}, bf16[256,128,4,128]{3,2,1,0:T(4,128)(2,1)}...) fusion(pred[256,128]{1,0:T(8,128)(4,1)} %get-tuple-element.97, ...), kind=kLoop, calls=%fused_computation.22 | loop fusion | flops 100663296 | bytes 270106624 | tf_op jit(solution)/shard_map/jit(_where)/select_n | solution.py:31
  265.7 21.1 %fusion.9 = f32[256,4,1,128]{3,2,1,0:T(1,128)S(1)} fusion(bf16[256,128,4,128]{3,2,1,0:T(4,128)(2,1)} %get-tuple-element.39, bf16[256,4,128,1]{2,1,0,3:T(4,128)(2,1)S(1)} %maximum_bitcast_fusion.1), kind=kOutput, calls=%fused_computation.15 | convolution fusion | flops 33554432 | bytes 34340864 | tf_op jit(solution)/shard_map/bkgh,bskh->bkgs/dot_general | solution.py:36
  288.2 21.1 %fusion.13 = f32[256,4,1,128]{3,2,1,0:T(1,128)S(1)} fusion(bf16[256,128,4,128]{3,2,1,0:T(4,128)(2,1)} %get-tuple-element.40, bf16[256,4,128,1]{2,1,0,3:T(4,128)(2,1)S(1)} %maximum_bitcast_fusion), kind=kOutput, calls=%fused_computation.19 | convolution fusion | flops 33554432 | bytes 34340864 | tf_op jit(solution)/shard_map/bkgh,bskh->bkgs/dot_general | solution.py:36
  309.9 14.8 %fusion.7 = f32[256,4,1,128]{3,2,1,0:T(1,128)S(1)} fusion(bf16[256,128,4,128]{3,2,1,0:T(4,128)(2,1)} %get-tuple-element.72, bf16[256,4,128,1]{2,0,1,3:T(8,128)(2,1)S(1)} %get-tuple-element.54), kind=kOutput, calls=%fused_computation.13 | convolution fusion | flops 33554432 | bytes 34340864 | tf_op jit(solution)/shard_map/bkgs,bskh->bkgh/dot_general | solution.py:42
  325.1 0.9 convolution_convert_fusion.10
  326.0 14.6 %fusion.11 = f32[256,4,1,128]{3,2,1,0:T(1,128)S(1)} fusion(bf16[256,128,4,128]{3,2,1,0:T(4,128)(2,1)} %get-tuple-element.73, bf16[256,4,128,1]{2,0,1,3:T(8,128)(2,1)S(1)} %get-tuple-element.58), kind=kOutput, calls=%fused_computation.17 | convolution fusion | flops 33554432 | bytes 34340864 | tf_op jit(solution)/shard_map/bkgs,bskh->bkgh/dot_general | solution.py:42
  341.0 0.9 convolution_convert_fusion.11
  342.7 21.1 %fusion.5 = f32[256,4,1,128]{3,2,1,0:T(1,128)S(1)} fusion(bf16[256,128,4,128]{3,2,1,0:T(4,128)(2,1)} %get-tuple-element.38, bf16[256,4,128,1]{2,1,0,3:T(4,128)(2,1)S(1)} %maximum_bitcast_fusion.2), kind=kOutput, calls=%fused_computation.11 | convolution fusion | flops 33554432 | bytes 34340864 | tf_op jit(solution)/shard_map/bkgh,bskh->bkgs/dot_general | solution.py:36
  364.5 14.8 %fusion.3 = f32[256,4,1,128]{3,2,1,0:T(1,128)S(1)} fusion(bf16[256,128,4,128]{3,2,1,0:T(4,128)(2,1)} %get-tuple-element.71, bf16[256,4,128,1]{2,0,1,3:T(8,128)(2,1)S(1)} %get-tuple-element.62), kind=kOutput, calls=%fused_computation.9 | convolution fusion | flops 33554432 | bytes 34340864 | tf_op jit(solution)/shard_map/bkgs,bskh->bkgh/dot_general | solution.py:42
  379.6 0.9 convolution_convert_fusion.9
  380.7 36.7 %all-reduce.21.cloned.1.call-done = (bf16[256,256]{1,0:T(8,128)(2,1)}, bf16[256,256]{1,0:T(8,128)(2,1)}, bf16[256,256]{1,0:T(8,128)(2,1)}) async-done(((bf16[256,256]{1,0:T(8,128)(2,1)}, bf16[256,256]{1,0:T(8,128)(2,1)}, bf16[256,256]{1,0:T(8,128)(2,1)}), (bf16[256,256]{1,0:T(8,128)(2,1)}, bf16[256,256]{1,0:T(8,128)(2,1)}, bf16[256,256]{1,0:T(8,128)(2,1)})) %all-reduce.21.cloned.1.call-update) | async-done | bytes 393232 | tf_op jit(solution)/shard_map/psum | solution.py:80
  417.4 1.1 fusion.125
  418.5 1.1 fusion.109
  419.7 1.1 fusion.117
  420.9 14.9 %all-reduce = (f32[256,1]{0,1:T(1,128)S(1)}, f32[256,1]{0,1:T(1,128)S(1)}, f32[256,1]{0,1:T(1,128)S(1)}) all-reduce(f32[256,1]{0,1:T(1,128)S(1)} %bitcast.300, f32[256,1]{0,1:T(1,128)S(1)} %bitcast.301, f32[256,1]{0,1:T(1,128)S(1)} %bitcast.302), channel_id=1, replica_groups=mesh['dp'=1,'y'=4,'x'=8] {'x'}, use_global_device_ids=true, to_apply=%region_35.38 | all-reduce | flops 768 | bytes 6144 | tf_op jit(solution)/shard_map/psum | solution.py:12
  435.8 0.9 fusion.185
  436.6 9.2 convert_bitcast_fusion.3
  445.8 0.9 fusion.189
  446.7 9.4 convert_bitcast_fusion.5
  456.1 5.6 convert_bitcast_fusion.2
  461.8 5.6 convert_bitcast_fusion.4
  467.4 0.9 fusion.181
  468.3 9.2 convert_bitcast_fusion.1
  477.4 9.4 convert_bitcast_fusion
  486.9 11.5 %pad_maximum_fusion.1 = bf16[2,64,256,256]{3,2,1,0:T(8,128)(2,1)} fusion(bf16[1,64,256,256]{3,2,1,0:T(8,128)(2,1)} %convert_bitcast_fusion.2, bf16[1,64,256,256]{3,2,1,0:T(8,128)(2,1)S(1)} %bitcast.276), kind=kLoop, calls=%fused_computation.49 | loop fusion | flops 8388608 | bytes 33554432 | tf_op jit(solution)/shard_map/stack | solution.py:85
  498.4 10.5 pad_maximum_fusion
  509.0 13.8 %pad_maximum_fusion.2 = bf16[2,64,256,256]{3,2,1,0:T(8,128)(2,1)} fusion(bf16[1,64,256,256]{3,2,1,0:T(8,128)(2,1)} %convert_bitcast_fusion, bf16[1,64,256,256]{3,2,1,0:T(8,128)(2,1)} %convert_bitcast_fusion.1), kind=kLoop, calls=%fused_computation.50 | loop fusion | flops 8388608 | bytes 33554432 | tf_op jit(solution)/shard_map/stack | solution.py:85
  524.3 36.2 %all-reduce.13.cloned.1.call-done = (f32[256,64]{0,1:T(8,128)}, f32[256,64]{0,1:T(8,128)}, f32[256,64]{0,1:T(8,128)}) async-done(((f32[256,64]{0,1:T(8,128)}, f32[256,64]{0,1:T(8,128)}, f32[256,64]{0,1:T(8,128)}), (f32[256,64]{0,1:T(8,128)}, f32[256,64]{0,1:T(8,128)}, f32[256,64]{0,1:T(8,128)})) %all-reduce.13.cloned.1.call-update) | async-done | bytes 196624 | tf_op jit(solution)/shard_map/psum | solution.py:83
  560.6 15.1 %gather_fusion.5 = f32[2048]{0:T(1024)S(1)} fusion(f32[256,64]{0,1:T(8,128)} %get-tuple-element.18, s32[2048]{0:T(1024)S(1)} %reshape.742), kind=kCustom, calls=%fused_computation.5.clone | custom fusion | bytes 32768 | tf_op jit(solution)/shard_map/jit(take_along_axis)/gather | solution.py:47
  575.9 0.7 copy-done.3
  576.6 16.8 %gather_fusion.1 = f32[2048]{0:T(1024)S(1)} fusion(f32[256,64]{0,1:T(8,128)S(1)} %copy-done.3, s32[2048]{0:T(1024)S(1)} %reshape.728), kind=kCustom, calls=%fused_computation.1.clone | custom fusion | bytes 32768 | tf_op jit(solution)/shard_map/jit(take_along_axis)/gather | solution.py:47
  593.5 0.7 copy-done.2
  594.2 16.8 %gather_fusion.3 = f32[2048]{0:T(1024)S(1)} fusion(f32[256,64]{0,1:T(8,128)S(1)} %copy-done.2, s32[2048]{0:T(1024)S(1)} %reshape.735), kind=kCustom, calls=%fused_computation.4.clone | custom fusion | bytes 32768 | tf_op jit(solution)/shard_map/jit(take_along_axis)/gather | solution.py:47
  611.4 445.3 %all-reduce.15.cloned.1.call-done = (bf16[2,64,256,256]{3,2,1,0:T(8,128)(2,1)}, bf16[2,64,256,256]{3,2,1,0:T(8,128)(2,1)}, bf16[2,64,256,256]{3,2,1,0:T(8,128)(2,1)}) async-done(((bf16[2,64,256,256]{3,2,1,0:T(8,128)(2,1)}, bf16[2,64,256,256]{3,2,1,0:T(8,128)(2,1)}, bf16[2,64,256,256]{3,2,1,0:T(8,128)(2,1)}), (bf16[2,64,256,256]{3,2,1,0:T(8,128)(2,1)}, bf16[2,64,256,256]{3,2,1,0:T(8,128)(2,1)}, ...) | async-done | bytes 50331664 | tf_op jit(solution)/shard_map/psum | solution.py:86
  1056.7 13.6 %fusion.63 = bf16[256,256]{1,0:T(8,128)(2,1)} fusion(bf16[64,256,256]{2,1,0:T(8,128)(2,1)} %param.35, bf16[2,64,256,256]{3,2,1,0:T(8,128)(2,1)} %get-tuple-element.20, f32[64,256]{1,0:T(8,128)S(1)} %bitcast.289), kind=kOutput, calls=%fused_computation.95 | convolution fusion | flops 2185297920 | bytes 25362432 | tf_op jit(solution)/shard_map/ebf,efd->bd/dot_general | solution.py:88
  1070.3 11.6 %fusion.60 = bf16[256,256]{1,0:T(8,128)(2,1)} fusion(bf16[64,256,256]{2,1,0:T(8,128)(2,1)} %param.35, bf16[2,64,256,256]{3,2,1,0:T(8,128)(2,1)S(1)} %copy-done.28, f32[64,256]{1,0:T(8,128)S(1)} %bitcast.290), kind=kOutput, calls=%fused_computation.94 | convolution fusion | flops 2185297920 | bytes 25362432 | tf_op jit(solution)/shard_map/ebf,efd->bd/dot_general | solution.py:88
  1082.1 10.1 fusion.57
  1092.2 35.4 %all-reduce.19.cloned.1.call-done = (bf16[256,256]{1,0:T(8,128)(2,1)}, bf16[256,256]{1,0:T(8,128)(2,1)}, bf16[256,256]{1,0:T(8,128)(2,1)}) async-done(((bf16[256,256]{1,0:T(8,128)(2,1)}, bf16[256,256]{1,0:T(8,128)(2,1)}, bf16[256,256]{1,0:T(8,128)(2,1)}), (bf16[256,256]{1,0:T(8,128)(2,1)}, bf16[256,256]{1,0:T(8,128)(2,1)}, bf16[256,256]{1,0:T(8,128)(2,1)})) %all-reduce.19.cloned.1.call-update) | async-done | bytes 393232 | tf_op jit(solution)/shard_map/psum | solution.py:88
  1127.7 0.9 fusion.152
  1128.6 0.9 fusion.150
  1129.6 0.9 fusion.151
  1130.5 0.8 pad_maximum_fusion.6
  (179 shorter events, 12.1 us)
Async XLA Ops:
  7.2 54.4 %copy-start = (bf16[256,512]{1,0:T(8,128)(2,1)S(1)}, bf16[256,512]{1,0:T(8,128)(2,1)}, u32[]{:S(2)}) copy-start(bf16[256,512]{1,0:T(8,128)(2,1)} %param.28) | copy-start | bytes 786436
  7.2 65.6 %copy-start.21 = (s32[256]{0:T(256)S(1)}, s32[256]{0:T(256)}, u32[]{:S(2)}) copy-start(s32[256]{0:T(256)} %param.21) | copy-start | bytes 3076
  7.2 127.6 %all-reduce.17.cloned.1.call-start = ((), (), s32[]{:S(2)}) async-start(), calls=%async_computation.2 | async-start | bytes 4718592 | tf_op jit(solution)/shard_map/psum | solution.py:73
  8.1 126.7 %copy-start.22 = (pred[256]{0:T(512)(128)(4,1)}, pred[256]{0:T(512)(128)(4,1)S(1)}, u32[]{:S(2)}) copy-start(pred[256]{0:T(512)(128)(4,1)S(1)} %compare_and_fusion.2) | copy-start | bytes 772
  8.1 126.7 %copy-start.26 = (pred[256]{0:T(512)(128)(4,1)}, pred[256]{0:T(512)(128)(4,1)S(1)}, u32[]{:S(2)}) copy-start(pred[256]{0:T(512)(128)(4,1)S(1)} %compare_and_fusion) | copy-start | bytes 772
  8.2 126.7 %copy-start.24 = (pred[256]{0:T(512)(128)(4,1)}, pred[256]{0:T(512)(128)(4,1)S(1)}, u32[]{:S(2)}) copy-start(pred[256]{0:T(512)(128)(4,1)S(1)} %compare_and_fusion.1) | copy-start | bytes 772
  21.5 118.0 %copy-start.13 = (bf16[256,256]{1,0:T(8,128)(2,1)}, bf16[256,256]{1,0:T(8,128)(2,1)S(1)}, u32[]{:S(2)}) copy-start(bf16[256,256]{1,0:T(8,128)(2,1)S(1)} %gather_fusion) | copy-start | bytes 393220
  34.1 103.3 %copy-start.15 = (bf16[256,256]{1,0:T(8,128)(2,1)}, bf16[256,256]{1,0:T(8,128)(2,1)S(1)}, u32[]{:S(2)}) copy-start(bf16[256,256]{1,0:T(8,128)(2,1)S(1)} %gather_fusion.4) | copy-start | bytes 393220
  46.8 92.7 %copy-start.11 = (bf16[256,256]{1,0:T(8,128)(2,1)}, bf16[256,256]{1,0:T(8,128)(2,1)S(1)}, u32[]{:S(2)}) copy-start(bf16[256,256]{1,0:T(8,128)(2,1)S(1)} %gather_fusion.2) | copy-start | bytes 393220
  72.7 344.7 %all-reduce.21.cloned.1.call-start = ((), (), s32[]{:S(2)}) async-start(), calls=%async_computation.4 | async-start | bytes 786432 | tf_op jit(solution)/shard_map/psum | solution.py:80
  265.6 21.1 %copy-start.20 = (pred[256,128]{1,0:T(8,128)(4,1)S(1)}, pred[256,128]{1,0:T(8,128)(4,1)}, u32[]{:S(2)}) copy-start(pred[256,128]{1,0:T(8,128)(4,1)} %get-tuple-element.108) | copy-start | bytes 98308
  288.2 21.1 %copy-start.18 = (pred[256,128]{1,0:T(8,128)(4,1)S(1)}, pred[256,128]{1,0:T(8,128)(4,1)}, u32[]{:S(2)}) copy-start(pred[256,128]{1,0:T(8,128)(4,1)} %get-tuple-element.94) | copy-start | bytes 98308
  309.9 15.2 %copy-start.4 = (bf16[512,256]{1,0:T(8,128)(2,1)S(1)}, bf16[512,256]{1,0:T(8,128)(2,1)}, u32[]{:S(2)}) copy-start(bf16[512,256]{1,0:T(8,128)(2,1)} %param.30) | copy-start | bytes 786436
  342.7 21.1 %copy-start.19 = (pred[256,128]{1,0:T(8,128)(4,1)S(1)}, pred[256,128]{1,0:T(8,128)(4,1)}, u32[]{:S(2)}) copy-start(pred[256,128]{1,0:T(8,128)(4,1)} %get-tuple-element.96) | copy-start | bytes 98308
  364.4 16.2 %copy-start.30 = (bf16[256]{0:T(256)(128)(2,1)S(1)}, bf16[256]{0:T(256)(128)(2,1)}, u32[]{:S(2)}) copy-start(bf16[256]{0:T(256)(128)(2,1)} %param.31) | copy-start | bytes 1540
  364.4 53.0 %copy-start.16 = (bf16[256,256]{1,0:T(8,128)(2,1)S(1)}, bf16[256,256]{1,0:T(8,128)(2,1)}, u32[]{:S(2)}) copy-start(bf16[256,256]{1,0:T(8,128)(2,1)} %copy-done.15) | copy-start | bytes 393220
  364.4 53.0 %copy-start.27 = (pred[256]{0:T(512)(128)(4,1)S(1)}, pred[256]{0:T(512)(128)(4,1)}, u32[]{:S(2)}) copy-start(pred[256]{0:T(512)(128)(4,1)} %copy-done.26) | copy-start | bytes 772
  364.4 54.1 %copy-start.14 = (bf16[256,256]{1,0:T(8,128)(2,1)S(1)}, bf16[256,256]{1,0:T(8,128)(2,1)}, u32[]{:S(2)}) copy-start(bf16[256,256]{1,0:T(8,128)(2,1)} %copy-done.13) | copy-start | bytes 393220
  364.4 54.1 %copy-start.23 = (pred[256]{0:T(512)(128)(4,1)S(1)}, pred[256]{0:T(512)(128)(4,1)}, u32[]{:S(2)}) copy-start(pred[256]{0:T(512)(128)(4,1)} %copy-done.22) | copy-start | bytes 772
  364.5 55.2 %copy-start.12 = (bf16[256,256]{1,0:T(8,128)(2,1)S(1)}, bf16[256,256]{1,0:T(8,128)(2,1)}, u32[]{:S(2)}) copy-start(bf16[256,256]{1,0:T(8,128)(2,1)} %copy-done.11) | copy-start | bytes 393220
  364.5 55.2 %copy-start.25 = (pred[256]{0:T(512)(128)(4,1)S(1)}, pred[256]{0:T(512)(128)(4,1)}, u32[]{:S(2)}) copy-start(pred[256]{0:T(512)(128)(4,1)} %copy-done.24) | copy-start | bytes 772
  364.5 71.3 %copy-start.29 = (bf16[256,64]{0,1:T(8,128)(2,1)S(1)}, bf16[256,64]{0,1:T(8,128)(2,1)}, u32[]{:S(2)}) copy-start(bf16[256,64]{0,1:T(8,128)(2,1)} %param.32) | copy-start | bytes 98308
  380.6 180.0 %all-reduce.13.cloned.1.call-start = ((), (), s32[]{:S(2)}) async-start(), calls=%async_computation | async-start | bytes 393216 | tf_op jit(solution)/shard_map/psum | solution.py:83
  418.5 58.9 %copy-start.5 = (bf16[256,256]{1,0:T(8,128)(2,1)}, bf16[256,256]{1,0:T(8,128)(2,1)S(1)}, u32[]{:S(2)}) copy-start(bf16[256,256]{1,0:T(8,128)(2,1)S(1)} %get-tuple-element.37) | copy-start | bytes 393220
  419.7 42.1 %copy-start.7 = (bf16[256,256]{1,0:T(8,128)(2,1)}, bf16[256,256]{1,0:T(8,128)(2,1)S(1)}, u32[]{:S(2)}) copy-start(bf16[256,256]{1,0:T(8,128)(2,1)S(1)} %get-tuple-element.35) | copy-start | bytes 393220
  420.9 35.2 %copy-start.9 = (bf16[256,256]{1,0:T(8,128)(2,1)}, bf16[256,256]{1,0:T(8,128)(2,1)S(1)}, u32[]{:S(2)}) copy-start(bf16[256,256]{1,0:T(8,128)(2,1)S(1)} %get-tuple-element.33) | copy-start | bytes 393220
  436.6 19.5 %slice-start = ((s8[8388608]{0:T(1024)(128)(4,1)}), s8[4194304]{0:T(1024)(128)(4,1)S(1)}, s32[]{:S(2)}) async-start(s8[8388608]{0:T(1024)(128)(4,1)} %bitcast.273), calls=%async_computation.5 | async-start | bytes 8388608
  445.8 10.3 slice-start.1
  468.3 18.6 %slice-start.2 = ((s8[8388608]{0:T(1024)(128)(4,1)}), s8[4194304]{0:T(1024)(128)(4,1)S(1)}, s32[]{:S(2)}) async-start(s8[8388608]{0:T(1024)(128)(4,1)} %bitcast.275), calls=%async_computation.7 | async-start | bytes 8388608
  477.4 9.4 slice-start.3
  477.4 21.0 %slice-start.4 = ((s8[8388608]{0:T(1024)(128)(4,1)}), s8[4194304]{0:T(1024)(128)(4,1)S(1)}, s32[]{:S(2)}) async-start(s8[8388608]{0:T(1024)(128)(4,1)} %bitcast.277), calls=%async_computation.9 | async-start | bytes 8388608
  486.9 11.5 %slice-start.5 = ((s8[8388608]{0:T(1024)(128)(4,1)}), s8[4194304]{0:T(1024)(128)(4,1)S(1)}, s32[]{:S(2)}) async-start(s8[8388608]{0:T(1024)(128)(4,1)} %bitcast.277), calls=%async_computation.10 | async-start | bytes 8388608
  508.9 547.8 %all-reduce.15.cloned.1.call-start = ((), (), s32[]{:S(2)}) async-start(), calls=%async_computation.1 | async-start | bytes 100663296 | tf_op jit(solution)/shard_map/psum | solution.py:86
  522.8 0.7 copy-start.17
  522.9 604.8 %all-reduce.19.cloned.1.call-start = ((), (), s32[]{:S(2)}) async-start(), calls=%async_computation.3 | async-start | bytes 786432 | tf_op jit(solution)/shard_map/psum | solution.py:88
  575.7 0.8 copy-start.3
  593.3 0.8 copy-start.2
  1056.7 13.6 %copy-start.28 = (bf16[2,64,256,256]{3,2,1,0:T(8,128)(2,1)S(1)}, bf16[2,64,256,256]{3,2,1,0:T(8,128)(2,1)}, u32[]{:S(2)}) copy-start(bf16[2,64,256,256]{3,2,1,0:T(8,128)(2,1)} %get-tuple-element.21) | copy-start | bytes 50331652
  1056.7 25.3 %slice-start.6 = ((s8[16777216]{0:T(1024)(128)(4,1)}), s8[4194304]{0:T(1024)(128)(4,1)S(1)}, s32[]{:S(2)}) async-start(s8[16777216]{0:T(1024)(128)(4,1)} %bitcast.321), calls=%async_computation.11 | async-start | bytes 8388608
  1056.7 25.3 %slice-start.7 = ((s8[16777216]{0:T(1024)(128)(4,1)}), s8[4194304]{0:T(1024)(128)(4,1)S(1)}, s32[]{:S(2)}) async-start(s8[16777216]{0:T(1024)(128)(4,1)} %bitcast.321), calls=%async_computation.12 | async-start | bytes 8388608
  1070.3 11.7 %slice-start.8 = ((s8[16777216]{0:T(1024)(128)(4,1)}), s8[4194304]{0:T(1024)(128)(4,1)S(1)}, s32[]{:S(2)}) async-start(s8[16777216]{0:T(1024)(128)(4,1)} %bitcast.321), calls=%async_computation.13 | async-start | bytes 8388608
  1070.3 11.7 %slice-start.9 = ((s8[16777216]{0:T(1024)(128)(4,1)}), s8[4194304]{0:T(1024)(128)(4,1)S(1)}, s32[]{:S(2)}) async-start(s8[16777216]{0:T(1024)(128)(4,1)} %bitcast.321), calls=%async_computation.14 | async-start | bytes 8388608
  1082.0 45.7 %copy-start.8 = (bf16[256,256]{1,0:T(8,128)(2,1)S(1)}, bf16[256,256]{1,0:T(8,128)(2,1)}, u32[]{:S(2)}) copy-start(bf16[256,256]{1,0:T(8,128)(2,1)} %copy-done.7) | copy-start | bytes 393220
  1082.0 46.6 %copy-start.6 = (bf16[256,256]{1,0:T(8,128)(2,1)S(1)}, bf16[256,256]{1,0:T(8,128)(2,1)}, u32[]{:S(2)}) copy-start(bf16[256,256]{1,0:T(8,128)(2,1)} %copy-done.5) | copy-start | bytes 393220
  1082.0 47.5 %copy-start.10 = (bf16[256,256]{1,0:T(8,128)(2,1)S(1)}, bf16[256,256]{1,0:T(8,128)(2,1)}, u32[]{:S(2)}) copy-start(bf16[256,256]{1,0:T(8,128)(2,1)} %copy-done.9) | copy-start | bytes 393220
  1082.1 49.3 %copy-start.1 = (bf16[256,512]{1,0:T(8,128)(2,1)S(1)}, bf16[256,512]{1,0:T(8,128)(2,1)}, u32[]{:S(2)}) copy-start(bf16[256,512]{1,0:T(8,128)(2,1)} %param.28) | copy-start | bytes 786436
Sparse Core Ops, SparseCore 0:
  72.8 61.9 all-reduce.16
  380.7 36.6 all-reduce.20
  509.1 51.4 all-reduce.12
  563.2 493.4 all-reduce.14
  1092.4 35.2 all-reduce.18
where the time goes:
time: 1150 us; the launch traced here: 1140 us
  waiting for transfers between devices  613 us (53%)
  matrix products  205 us (18%)
  other arithmetic  180 us (16%)
  local copies, waits for them, and re-layouts  96.5 us (8%)
  blocking collectives  28.7 us (2%)
  between operations  15.3 us (1%)
    psum x1, waiting for transfers between devices, per_device(): hidden_sum = lax.psum(hidden_part, 'x')  445 us
    select_n x1, other arithmetic, write_slot(): return jnp.where(hit_mask, new_rows[:, None], cache_arr)  125 us
    dot_general x3, matrix products, attention(): jnp.einsum('bkgh,bskh->bkgs', queries, key_cache, preferred_element_type=...  63.2 us
    psum x1, waiting for transfers between devices, per_device(): proj_sum = lax.psum(proj_part, 'x')  59.1 us
    gather x15, local copies, waits for them, and re-layouts, mixing(): jnp.take_along_axis(logits, choice_row, axis=1)  49.9 us
    dot_general x3, matrix products, attention(): jnp.einsum('bkgs,bskh->bkgh', weight.astype(jnp.bfloat16), val_cache, pre...  44.2 us
    gather x3, local copies, waits for them, and re-layouts, per_device(): x_in = jnp.take(emb_table, tokens[step_idx], axis=0)  37.9 us
    psum x1, waiting for transfers between devices, per_device(): lax.psum(jnp.dot(mixed, w_o, preferred_element_type=jnp.float32).astype(j...  36.7 us
  transfers between devices with their start and end apart: 5, of which 5 were waited for; matrix products, arithmetic and copies ran while one was open for 6% of the time, Pallas kernels for 0%

commit v1 on v0

v1 whole, which is shorter than its diff:
```python
import functools

import jax
import jax.numpy as jnp
from jax import lax
from jax.experimental import pallas as pl
from jax.experimental.pallas import tpu as pltpu
from jax.sharding import PartitionSpec as P

EPS = 1e-5
ROPE_BASE = 1.0e6
TILE = 128
BF16 = jnp.bfloat16
F32 = jnp.float32


def shard_norm(x_val, gain_vec, width_full):
    x_f32 = x_val.astype(F32)
    sq_total = lax.psum(jnp.sum(x_f32 * x_f32, axis=-1, keepdims=True), 'x')
    return (x_f32 * lax.rsqrt(sq_total / width_full + EPS) * gain_vec.astype(F32)).astype(BF16)


def rotate(vectors, positions):
    head_dim = vectors.shape[-1]
    half_dim = head_dim // 2
    inv_freq = ROPE_BASE ** (-(jnp.arange(half_dim, dtype=F32) * 2.0 / head_dim))
    angles = (positions.astype(F32)[:, None] * inv_freq[None, :])[:, None, :]
    cosine = jnp.cos(angles)
    sine_val = jnp.sin(angles)
    first_half = vectors[..., :half_dim].astype(F32)
    second_half = vectors[..., half_dim:].astype(F32)
    return jnp.concatenate([first_half * cosine - second_half * sine_val, second_half * cosine + first_half * sine_val], axis=-1).astype(BF16)


def attention(queries, key_cache, val_cache, positions):
    head_dim = queries.shape[-1]
    scores = jnp.einsum('tbkh,bskh->bkts', queries, key_cache, preferred_element_type=F32) * head_dim ** -0.5
    valid_mask = (jnp.arange(key_cache.shape[1])[None, None, :] <= positions.T[:, :, None])[:, None]
    scores = jnp.where(valid_mask, scores, -1.0e30)
    peak_val = jnp.max(scores, axis=-1, keepdims=True)
    weight = jnp.where(valid_mask, jnp.exp(scores - peak_val), 0.0)
    total_w = jnp.sum(weight, axis=-1, keepdims=True)
    mixed_out = jnp.einsum('bkts,bskh->bkth', weight.astype(BF16), val_cache, preferred_element_type=F32)
    return (mixed_out / total_w).astype(BF16).transpose(2, 0, 1, 3)


def write_slots(cache_arr, new_rows, lengths):
    slots = jnp.arange(cache_arr.shape[1])[None, :]
    for step_idx in range(new_rows.shape[0]):
        hit_mask = (slots == (lengths + step_idx)[:, None])[:, :, None, None]
        cache_arr = jnp.where(hit_mask, new_rows[step_idx][:, None], cache_arr)
    return cache_arr


def up_kernel(per_step, tile, off_ref, pos_ref, h_ref, act_ref, lin_ref, out_ref):
    step = pl.program_id(0)

    @pl.when(step == 0)
    def _():
        out_ref[...] = jnp.zeros_like(out_ref)

    tokens = h_ref.shape[0]
    width = act_ref.shape[2]
    row_iota = lax.broadcasted_iota(jnp.int32, (tile, tokens), 0)
    for j in range(per_step):
        e = step * per_step + j
        lo, hi = off_ref[e], off_ref[e + 1]
        pos_row = pos_ref[j]

        def visit(i, carry):
            base = pl.multiple_of(i * tile, tile)
            pick = (jnp.broadcast_to(pos_row - base, (tile, tokens)) == row_iota).astype(F32).astype(BF16)
            rows = jnp.dot(pick, h_ref[...], preferred_element_type=F32).astype(BF16)
            act = jnp.dot(rows, act_ref[j], preferred_element_type=F32).astype(BF16)
            lin = jnp.dot(rows, lin_ref[j], preferred_element_type=F32).astype(BF16)
            out_ref[pl.ds(base, tile), :width] += act
            out_ref[pl.ds(base, tile), width:] += lin
            return carry

        lax.fori_loop(lo // tile, (hi + tile - 1) // tile, visit, 0)


def down_kernel(per_step, tile, off_ref, pos_ref, u_ref, w_ref, out_ref, acc_ref, mix_ref):
    step = pl.program_id(0)

    @pl.when(step == 0)
    def _():
        acc_ref[...] = jnp.zeros_like(acc_ref)

    tokens = out_ref.shape[0]
    row_iota = lax.broadcasted_iota(jnp.int32, (tile, tokens), 0)
    for j in range(per_step):
        e = step * per_step + j
        lo, hi = off_ref[e], off_ref[e + 1]
        pos_row = pos_ref[j]
        mix_ref[...] = jnp.zeros_like(mix_ref)

        def visit(i, carry):
            base = pl.multiple_of(i * tile, tile)
            pick = (jnp.broadcast_to(pos_row - base, (tile, tokens)) == row_iota).astype(F32).astype(BF16)
            mix_ref[...] += lax.dot_general(pick, u_ref[pl.ds(base, tile), :], (((0,), (0,)), ((), ())), preferred_element_type=F32).astype(BF16)
            return carry

        lax.fori_loop(lo // tile, (hi + tile - 1) // tile, visit, 0)
        acc_ref[...] += jnp.dot(mix_ref[...], w_ref[j], preferred_element_type=F32)

    @pl.when(step == pl.num_programs(0) - 1)
    def _():
        out_ref[...] = acc_ref[...].astype(BF16)


def experts_up(offsets, pos_rows, normed, w_act, w_lin, pairs):
    experts, depth, width = w_act.shape
    tokens = normed.shape[0]
    per_step = 4
    return pl.pallas_call(
        functools.partial(up_kernel, per_step, TILE),
        out_shape=jax.ShapeDtypeStruct((pairs, 2 * width), BF16),
        grid_spec=pltpu.PrefetchScalarGridSpec(
            num_scalar_prefetch=1,
            grid=(experts // per_step,),
            in_specs=[
                pl.BlockSpec((per_step, 1, tokens), lambda s, off: (s, 0, 0)),
                pl.BlockSpec((tokens, depth), lambda s, off: (0, 0)),
                pl.BlockSpec((per_step, depth, width), lambda s, off: (s, 0, 0)),
                pl.BlockSpec((per_step, depth, width), lambda s, off: (s, 0, 0)),
            ],
            out_specs=pl.BlockSpec((pairs, 2 * width), lambda s, off: (0, 0)),
        ),
        compiler_params=pltpu.CompilerParams(dimension_semantics=("arbitrary",), vmem_limit_bytes=48 << 20),
        cost_estimate=pl.CostEstimate(flops=12 << 30, bytes_accessed=24 << 20, transcendentals=0),
        name="experts_up",
    )(offsets, pos_rows, normed, w_act, w_lin)


def experts_down(offsets, pos_rows, unit, w_down):
    experts, width, depth = w_down.shape
    tokens = pos_rows.shape[2]
    per_step = 4
    return pl.pallas_call(
        functools.partial(down_kernel, per_step, TILE),
        out_shape=jax.ShapeDtypeStruct((tokens, depth), BF16),
        grid_spec=pltpu.PrefetchScalarGridSpec(
            num_scalar_prefetch=1,
            grid=(experts // per_step,),
            in_specs=[
                pl.BlockSpec((per_step, 1, tokens), lambda s, off: (s, 0, 0)),
                pl.BlockSpec(unit.shape, lambda s, off: (0, 0)),
                pl.BlockSpec((per_step, width, depth), lambda s, off: (s, 0, 0)),
            ],
            out_specs=pl.BlockSpec((tokens, depth), lambda s, off: (0, 0)),
            scratch_shapes=[pltpu.VMEM((tokens, depth), F32), pltpu.VMEM((tokens, width), BF16)],
        ),
        compiler_params=pltpu.CompilerParams(dimension_semantics=("arbitrary",), vmem_limit_bytes=40 << 20),
        cost_estimate=pl.CostEstimate(flops=12 << 30, bytes_accessed=12 << 20, transcendentals=0),
        name="experts_down",
    )(offsets, pos_rows, unit, w_down)


def solution(mesh):
    nx = mesh.shape['x']
    cache_spec = P('dp', None, 'y', None)
    in_specs = (P(None, 'dp'), P('dp'), P(None, 'dp', None), P(None, 'x'), cache_spec, cache_spec, P('x'), P('x', 'y'), P('x', 'y'), P('x', 'y'), P('y', 'x'), P('x'), P('x', None), P(None, 'x', 'y'), P(None, 'x', 'y'), P(None, 'y', 'x'))
    out_specs = (P(None, 'dp', 'x'), cache_spec, cache_spec)

    def per_device(tokens, lengths, choices, emb_table, k_cache, v_cache, g_attn, w_q, w_k, w_v, w_o, g_ffn, w_router, w_act, w_lin, w_down):
        steps, batch = tokens.shape
        top = choices.shape[2]
        heads, head_dim = k_cache.shape[2], k_cache.shape[3]
        cols = heads * head_dim
        width_full = emb_table.shape[1] * nx
        experts = w_act.shape[0]
        my_x = lax.axis_index('x')
        part = batch // nx
        rows = steps * batch
        pairs = rows * top

        def to_rows(arr):
            return arr.reshape((steps, nx, part) + arr.shape[2:]).swapaxes(0, 1).reshape((rows,) + arr.shape[2:])

        def from_rows(arr):
            return arr.reshape((nx, steps, part) + arr.shape[1:]).swapaxes(0, 1).reshape((steps, batch) + arr.shape[1:])

        choice_rows = to_rows(choices)
        member = jnp.any(choice_rows[:, :, None] == jnp.arange(experts)[None, None, :], axis=1)
        member_f = member.astype(F32)
        before = (jnp.arange(rows)[None, :] < jnp.arange(rows)[:, None]).astype(BF16)
        rank = jnp.dot(before, member.astype(BF16), preferred_element_type=F32)
        counts = jnp.sum(member_f, axis=0)
        ends = jnp.cumsum(counts)
        starts = ends - counts
        pos = jnp.where(member, rank + starts[None, :], -1.0)
        pos_rows = pos.T.astype(jnp.int32)[:, None, :]
        offsets = jnp.concatenate([starts, ends[-1:]]).astype(jnp.int32)
        share = pairs // nx
        own = (my_x * share + jnp.arange(share)).astype(F32)
        own_expert = ((own[:, None] >= starts[None, :]) & (own[:, None] < ends[None, :])).astype(F32)
        own_pos = lax.dot_general(own_expert, pos, (((1,), (1,)), ((), ())), precision=lax.Precision.HIGHEST, preferred_element_type=F32)
        own_token = (own_pos == own[:, None]).astype(F32)

        x_in = jnp.take(emb_table, to_rows(tokens), axis=0)
        normed = shard_norm(x_in, g_attn, width_full)
        proj_part = jnp.concatenate([jnp.dot(normed, w, preferred_element_type=F32).astype(BF16) for w in (w_q, w_k, w_v)], axis=1)
        proj = lax.psum_scatter(proj_part, 'x', scatter_dimension=0, tiled=True)
        my_lengths = lax.dynamic_slice_in_dim(lengths, my_x * part, part)
        my_positions = my_lengths[None, :] + jnp.arange(steps)[:, None]
        flat_positions = my_positions.reshape(-1)
        queries = rotate(proj[:, :cols].reshape(-1, heads, head_dim), flat_positions)
        new_keys = rotate(proj[:, cols:2 * cols].reshape(-1, heads, head_dim), flat_positions)
        new_vals = proj[:, 2 * cols:].reshape(-1, heads, head_dim)

        def split(arr):
            return arr.reshape(steps, part, heads, head_dim)

        my_keys = write_slots(lax.dynamic_slice_in_dim(k_cache, my_x * part, part), split(new_keys), my_lengths)
        my_vals = write_slots(lax.dynamic_slice_in_dim(v_cache, my_x * part, part), split(new_vals), my_lengths)
        mixed = attention(split(queries), my_keys, my_vals, my_positions).reshape(-1, cols)
        mixed_all = lax.all_gather(mixed, 'x', axis=0, tiled=True)

        new_kv = jnp.concatenate([new_keys.reshape(-1, cols), proj[:, 2 * cols:]], axis=1)
        kv_all = from_rows(lax.all_gather(new_kv, 'x', axis=0, tiled=True))
        k_out = write_slots(k_cache, kv_all[:, :, :cols].reshape(steps, batch, heads, head_dim), lengths)
        v_out = write_slots(v_cache, kv_all[:, :, cols:].reshape(steps, batch, heads, head_dim), lengths)

        attn_sum = lax.psum(jnp.dot(mixed_all, w_o, preferred_element_type=F32).astype(BF16), 'y')
        x_mid = (x_in.astype(F32) + attn_sum.astype(F32)).astype(BF16)
        normed2 = shard_norm(x_mid, g_ffn, width_full)
        logits = lax.psum(jnp.dot(normed2, w_router, preferred_element_type=F32), 'x')
        masked = jnp.where(member, logits, -jnp.inf)
        expd = jnp.exp(masked - jnp.max(masked, axis=1, keepdims=True))
        coef = expd / jnp.sum(expd, axis=1, keepdims=True)
        own_gate = jnp.sum(own_expert * jnp.dot(own_token, coef, precision=lax.Precision.HIGHEST, preferred_element_type=F32), axis=1, keepdims=True)

        hidden_part = experts_up(offsets, pos_rows, normed2, w_act, w_lin, pairs)
        hidden = lax.psum_scatter(hidden_part, 'x', scatter_dimension=0, tiled=True)
        width = w_act.shape[2]
        unit = (own_gate * jax.nn.silu(hidden[:, :width].astype(F32)) * hidden[:, width:].astype(F32)).astype(BF16)
        unit_all = lax.all_gather(unit, 'x', axis=0, tiled=True)
        moe_sum = lax.psum(experts_down(offsets, pos_rows, unit_all, w_down), 'y')
        hidden_out = (x_mid.astype(F32) + moe_sum.astype(F32)).astype(BF16)
        return from_rows(hidden_out), k_out, v_out

    return jax.shard_map(per_device, mesh=mesh, in_specs=in_specs, out_specs=out_specs, check_vma=False)
```

time: 1150 us -> 566 us (0.49); the launches traced: 1140 us -> 566 us
  waiting for transfers between devices: 613 us -> 205 us
  matrix products: 205 us -> 15.1 us
  Pallas kernels: 0 us -> 102 us
  local copies, waits for them, and re-layouts: 96.5 us -> 30.2 us
  other arithmetic: 180 us -> 147 us
  blocking collectives: 28.7 us -> 49.6 us
    psum x5 -> x3, waiting for transfers between devices: 613 us -> 90.8 us  [the longest x1 50.9 us: per_device(): lax.psum(jnp.dot(normed2, w_router, preferred_element_type=F32), 'x')]
    dot_general x30 -> x9, matrix products: 205 us -> 10.4 us  [the longest x1 3.41 us: attention(): jnp.einsum('bkts,bskh->bkth', weight.astype(BF16), val_cache, preferred_e...]
    pallas_call x0 -> x2, Pallas kernels: none -> 102 us  [the longest x1 51.6 us: experts_down(): pl.pallas_call(functools.partial(down_kernel, per_step, TILE), out_shape=...]
    gather x18 -> x1, local copies, waits for them, and re-layouts: 87.8 us -> 13.7 us  [per_device(): x_in = jnp.take(emb_table, to_rows(tokens), axis=0)]
    reduce_scatter x0 -> x2, waiting for transfers between devices: none -> 67.5 us  [the longest x1 37 us: per_device(): hidden = lax.psum_scatter(hidden_part, 'x', scatter_dimension=0, tiled=True)]
    all_gather x0 -> x2, waiting for transfers between devices: none -> 46.8 us  [the longest x1 25.1 us: per_device(): unit_all = lax.all_gather(unit, 'x', axis=0, tiled=True)]
    another operation x9 -> x3, other arithmetic: 39.7 us -> 0.26 us  [the longest x3 35.8 us: per_device(): jnp.stack([jnp.einsum('bd,edf->ebf', normed2, w_act, preferred_element_ty...]
    all_gather x0 -> x1, blocking collectives: none -> 21.2 us  [per_device(): mixed_all = lax.all_gather(mixed, 'x', axis=0, tiled=True)]
  transfers between devices with their start and end apart: 5 -> 7, of which waited for: 5 -> 6; matrix products, arithmetic and copies ran while one was open for 6% -> 23% of each run, Pallas kernels for 0% -> 0%
where the time goes in v1:
time: 566 us
  waiting for transfers between devices  205 us (36%)
  other arithmetic  147 us (26%)
  Pallas kernels  102 us (18%)
  blocking collectives  49.6 us (9%)
  local copies, waits for them, and re-layouts  30.2 us (5%)
  matrix products  15.1 us (3%)
  between operations  14.7 us (3%)
    select_n x2, other arithmetic, write_slots(): cache_arr = jnp.where(hit_mask, new_rows[step_idx][:, None], cache_arr)  137 us
    pallas_call x1, Pallas kernels, experts_down(): pl.pallas_call(functools.partial(down_kernel, per_step, TILE), out_shape=...  51.6 us
    psum x1, waiting for transfers between devices, per_device(): lax.psum(jnp.dot(normed2, w_router, preferred_element_type=F32), 'x')  50.9 us
    pallas_call x1, Pallas kernels, experts_up(): pl.pallas_call(functools.partial(up_kernel, per_step, TILE), out_shape=ja...  50.9 us
    psum x1, waiting for transfers between devices, per_device(): lax.psum(jnp.dot(mixed_all, w_o, preferred_element_type=F32).astype(BF16)...  39.9 us
    reduce_scatter x1, waiting for transfers between devices, per_device(): hidden = lax.psum_scatter(hidden_part, 'x', scatter_dimension=0, tiled=True)  37 us
    reduce_scatter x1, waiting for transfers between devices, per_device(): proj = lax.psum_scatter(proj_part, 'x', scatter_dimension=0, tiled=True)  30.4 us
    psum x2, blocking collectives, shard_norm(): sq_total = lax.psum(jnp.sum(x_f32 * x_f32, axis=-1, keepdims=True), 'x')  28.5 us
  transfers between devices with their start and end apart: 7, of which 6 were waited for; matrix products, arithmetic and copies ran while one was open for 23% of the time, Pallas kernels for 0%

profile of v1, /device:TPU:97, one launch (start us, length us, event | category | flops | bytes accessed | tf_op | source)
XLA Modules:
  0.0 565.9 jit_solution(7751943896618644593)
XLA Ops:
  7.3 0.8 reshape.368
  8.3 0.7 convert_element_type.116
  9.0 13.7 %gather_fusion = bf16[768,256]{1,0:T(8,128)(2,1)S(1)} fusion(bf16[50304,256]{1,0:T(8,128)(2,1)} %param.19, s32[1024]{0:T(1024)S(1)} %pad_clamp_fusion), kind=kCustom, calls=%fused_computation | custom fusion | bytes 789504 | tf_op jit(solution)/shard_map/jit(_take)/gather | solution.py:201
  22.7 0.3 fusion.41
  23.0 13.9 %psum.35 = f32[768,1]{0,1:T(1,128)S(1)} all-reduce(f32[768,1]{0,1:T(1,128)S(1)} %broadcast_in_dim.240), channel_id=1, replica_groups=mesh['dp'=1,'y'=4,'x'=8] {'x'}, use_global_device_ids=true, to_apply=%region_1.0 | all-reduce | flops 768 | bytes 6144 | tf_op jit(solution)/shard_map/psum | solution.py:19
  36.9 0.7 convolution_convert_fusion.1
  37.6 0.7 convolution_convert_fusion
  38.3 0.7 convolution_convert_fusion.2
  38.9 0.2 pad_maximum_fusion
  39.1 2.4 copy.136
  41.6 0.2 all-reduce.4.cloned.1.call-start
  42.3 0.1 iota_compare_fusion.10
  42.4 0.2 multiply_cosine_fusion
  42.6 30.4 %reduce-scatter.7.cloned.1.call-done = bf16[96,1536]{1,0:T(8,128)(2,1)} async-done(((bf16[768,1536]{1,0:T(8,128)(2,1)}), bf16[96,1536]{1,0:T(8,128)(2,1)}) %reduce-scatter.7.cloned.1.call-update) | async-done | bytes 294928 | tf_op jit(solution)/shard_map/reduce_scatter | solution.py:204
  73.0 0.8 fusion.78
  73.8 0.1 copy.140
  74.0 0.1 copy.122
  74.1 1.0 fusion.77
  75.1 0.1 copy.139
  75.2 0.1 copy.138
  75.5 0.1 copy.111
  75.7 0.1 copy.112
  75.8 0.1 copy.141
  76.1 0.1 copy.142
  76.4 0.1 fusion.79
  76.8 18.1 %select_select_fusion.3 = (bf16[32,128,4,128]{3,2,1,0:T(4,128)(2,1)}, bf16[32,128,4,128]{3,2,1,0:T(4,128)(2,1)}) fusion(bf16[256,128,4,128]{3,2,1,0:T(4,128)(2,1)} %param.20, s32[]{:T(128)S(6)} %select_n.82, pred[32,128]{1,0:T(8,128)(4,1)S(1)} %get-tuple-element.38, pred[32,128]{1,0:T(8,128)(4,1)S(1)} %iota_compare_fusion.12, ...), kind=kLoop, calls=%fused_computation.9 | loop fusion | flops 12582912 | bytes 16986116 | tf_op jit(solution)/shard_map/jit(_where)/select_n | solution.py:51
  94.9 4.7 fusion.80
  99.6 3.4 fusion.33
  103.1 21.2 %all_gather.9 = bf16[768,512]{1,0:T(8,128)(2,1)S(1)} all-gather(bf16[96,512]{1,0:T(8,128)(2,1)S(1)} %bitcast.67), channel_id=1, replica_groups=mesh['dp'=1,'y'=4,'x'=8] {'x'}, dimensions={0}, use_global_device_ids=true | all-gather | bytes 884736 | tf_op jit(solution)/shard_map/all_gather | solution.py:218
  124.3 1.1 convolution_convert_fusion.3
  125.7 0.1 eq.81
  125.9 39.9 %all-reduce.4.cloned.1.call-done = bf16[768,256]{1,0:T(8,128)(2,1)} async-done(((bf16[768,256]{1,0:T(8,128)(2,1)}), bf16[768,256]{1,0:T(8,128)(2,1)}) %all-reduce.4.cloned.1.call-update) | async-done | bytes 393232 | tf_op jit(solution)/shard_map/psum | solution.py:225
  165.8 1.4 fusion.45
  167.2 14.6 %psum.37 = f32[768,1]{0,1:T(1,128)S(1)} all-reduce(f32[768,1]{0,1:T(1,128)S(1)} %broadcast_in_dim.257), channel_id=1, replica_groups=mesh['dp'=1,'y'=4,'x'=8] {'x'}, use_global_device_ids=true, to_apply=%region_10.11 | all-reduce | flops 768 | bytes 6144 | tf_op jit(solution)/shard_map/psum | solution.py:19
  181.8 0.2 fusion.47.h_ref
  182.0 0.9 fusion.85
  183.1 0.2 fusion.8
  183.3 50.9 %all-reduce.6.cloned.1.call-done = f32[768,64]{0,1:T(8,128)} async-done(((f32[768,64]{0,1:T(8,128)}), f32[768,64]{0,1:T(8,128)}) %all-reduce.6.cloned.1.call-update) | async-done | bytes 196624 | tf_op jit(solution)/shard_map/psum | solution.py:228
  234.2 1.0 fusion.65
  235.2 1.1 fusion.51
  236.5 0.5 slice.130
  237.0 0.1 reduce.2
  237.1 0.4 fusion.26
  237.5 0.7 maximum_convert_fusion.1.off_ref
  238.2 0.1 broadcast_in_dim.256.pos_ref
  238.4 50.9 %experts_up.1 = bf16[6144,512]{1,0:T(8,128)(2,1)} custom-call(s32[65]{0:T(128)S(1)} %maximum_convert_fusion.1.off_ref, s32[64,1,768]{2,1,0:T(1,128)S(1)} %broadcast_in_dim.256.pos_ref, bf16[768,256]{1,0:T(8,128)(2,1)S(1)} %fusion.47.h_ref, bf16[64,256,256]{2,1,0:T(8,128)(2,1)} %act_ref.1, bf16[64,256,256]{2,1,0:T(8,128)(2,1)} %lin_ref.1), custom_call_target="tpu_custom_call" | custom-call | flops 12884901888 | bytes 25165824 | tf_op jit(solution)/shard_map/experts_up/pallas_call | solution.py:116
  289.4 0.1 copy.135
  289.5 0.7 pad_maximum_fusion.1
  290.3 0.3 all-gather.3.cloned.1.call-start
  290.6 1.2 fusion.52
  291.8 1.4 fusion.27
  293.2 37.0 %reduce-scatter.5.cloned.1.call-done = bf16[768,512]{1,0:T(8,128)(2,1)} async-done(((bf16[6144,512]{1,0:T(8,128)(2,1)}), bf16[768,512]{1,0:T(8,128)(2,1)}) %reduce-scatter.5.cloned.1.call-update) | async-done | bytes 786448 | tf_op jit(solution)/shard_map/reduce_scatter | solution.py:235
  330.2 2.2 fusion.49
  332.6 0.1 iota_compare_fusion.8
  332.8 21.7 %all-gather.5.cloned.1.call-done = bf16[768,1024]{1,0:T(8,128)(2,1)} async-done(((bf16[96,1024]{1,0:T(8,128)(2,1)}), bf16[768,1024]{1,0:T(8,128)(2,1)}) %all-gather.5.cloned.1.call-update) | async-done | bytes 1572880 | tf_op jit(solution)/shard_map/all_gather | solution.py:221
  354.5 1.6 copy.132
  356.1 0.1 fusion.76
  356.7 25.1 %all-gather.3.cloned.1.call-done.u_ref = bf16[6144,256]{1,0:T(8,128)(2,1)} async-done(((bf16[768,256]{1,0:T(8,128)(2,1)}), bf16[6144,256]{1,0:T(8,128)(2,1)}) %all-gather.3.cloned.1.call-update) | async-done | bytes 3145744 | tf_op jit(solution)/shard_map/all_gather | solution.py:238
  381.7 3.4 copy-done.2
  385.1 1.9 copy-done.3
  387.0 51.6 %experts_down.1 = bf16[768,256]{1,0:T(8,128)(2,1)} custom-call(s32[65]{0:T(128)S(1)} %maximum_convert_fusion.1.off_ref, s32[64,1,768]{2,1,0:T(1,128)S(1)} %broadcast_in_dim.256.pos_ref, bf16[6144,256]{1,0:T(8,128)(2,1)S(1)} %copy-done.3, bf16[64,256,256]{2,1,0:T(8,128)(2,1)S(1)} %copy-done.2), custom_call_target="tpu_custom_call" | custom-call | flops 12884901888 | bytes 12582912 | tf_op jit(solution)/shard_map/experts_down/pallas_call | solution.py:140
  438.6 118.5 %select_select_fusion = (bf16[256,128,4,128]{3,2,1,0:T(4,128)(2,1)}, bf16[256,128,4,128]{3,2,1,0:T(4,128)(2,1)}) fusion(bf16[256,128,4,128]{3,2,1,0:T(4,128)(2,1)} %param.21, pred[256,128]{1,0:T(8,128)(4,1)S(1)} %iota_compare_fusion.7, pred[256,128]{1,0:T(8,128)(4,1)S(1)} %get-tuple-element.40, pred[256,128]{1,0:T(8,128)(4,1)S(1)} %get-tuple-element.41, ...), kind=kLoop, calls=%fused_computation.2 | loop fusion | flops 100663296 | bytes 135888896 | tf_op jit(solution)/shard_map/jit(_where)/select_n | solution.py:51
  557.1 1.1 fusion.48
  558.2 0.8 copy.129
  (81 shorter events, 3.2 us)
Async XLA Ops:
  7.2 29.7 %copy-start = (bf16[256,512]{1,0:T(8,128)(2,1)S(1)}, bf16[256,512]{1,0:T(8,128)(2,1)}, u32[]{:S(2)}) copy-start(bf16[256,512]{1,0:T(8,128)(2,1)} %param.24) | copy-start | bytes 786436
  7.2 30.4 %copy-start.9 = (bf16[256,512]{1,0:T(8,128)(2,1)S(1)}, bf16[256,512]{1,0:T(8,128)(2,1)}, u32[]{:S(2)}) copy-start(bf16[256,512]{1,0:T(8,128)(2,1)} %param.25) | copy-start | bytes 786436
  7.2 31.1 %copy-start.10 = (bf16[256,512]{1,0:T(8,128)(2,1)S(1)}, bf16[256,512]{1,0:T(8,128)(2,1)}, u32[]{:S(2)}) copy-start(bf16[256,512]{1,0:T(8,128)(2,1)} %param.23) | copy-start | bytes 786436
  7.2 65.8 %reduce-scatter.7.cloned.1.call-start = ((), (), s32[]{:S(2)}) async-start(), calls=%async_computation.8 | async-start | bytes 2654208 | tf_op jit(solution)/shard_map/reduce_scatter | solution.py:204
  39.1 2.8 copy-start.8
  41.6 124.2 %all-reduce.4.cloned.1.call-start = ((), (), s32[]{:S(2)}) async-start(), calls=%async_computation.2 | async-start | bytes 786432 | tf_op jit(solution)/shard_map/psum | solution.py:225
  99.6 24.7 %copy-start.5 = (bf16[512,256]{1,0:T(8,128)(2,1)S(1)}, bf16[512,256]{1,0:T(8,128)(2,1)}, u32[]{:S(2)}) copy-start(bf16[512,256]{1,0:T(8,128)(2,1)} %param.26) | copy-start | bytes 786436
  99.6 25.9 %copy-start.11 = (bf16[256]{0:T(256)(128)(2,1)S(1)}, bf16[256]{0:T(256)(128)(2,1)}, u32[]{:S(2)}) copy-start(bf16[256]{0:T(256)(128)(2,1)} %param.27) | copy-start | bytes 1540
  99.6 25.9 %copy-start.7 = (s32[3,256,8]{1,2,0:T(8,128)S(1)}, s32[3,256,8]{1,2,0:T(8,128)}, u32[]{:S(2)}) copy-start(s32[3,256,8]{1,2,0:T(8,128)} %param.18) | copy-start | bytes 73732
  103.0 78.9 %copy-start.6 = (bf16[256,64]{0,1:T(8,128)(2,1)S(1)}, bf16[256,64]{0,1:T(8,128)(2,1)}, u32[]{:S(2)}) copy-start(bf16[256,64]{0,1:T(8,128)(2,1)} %param.28) | copy-start | bytes 98308
  125.5 108.7 %all-reduce.6.cloned.1.call-start = ((), (), s32[]{:S(2)}) async-start(), calls=%async_computation.3 | async-start | bytes 393216 | tf_op jit(solution)/shard_map/psum | solution.py:228
  183.0 147.2 %reduce-scatter.5.cloned.1.call-start = ((), (), s32[]{:S(2)}) async-start(), calls=%async_computation.4 | async-start | bytes 7077888 | tf_op jit(solution)/shard_map/reduce_scatter | solution.py:235
  289.3 2.5 copy-start.4
  289.3 65.2 %all-gather.5.cloned.1.call-start = ((), (), s32[]{:S(2)}) async-start(), calls=%async_computation.7 | async-start | bytes 1769472 | tf_op jit(solution)/shard_map/all_gather | solution.py:221
  290.3 91.4 %all-gather.3.cloned.1.call-start = ((), (), s32[]{:S(2)}) async-start(), calls=%async_computation.5 | async-start | bytes 3538944 | tf_op jit(solution)/shard_map/all_gather | solution.py:238
  332.5 224.7 %all-reduce.8.cloned.1.call-start = ((), (), s32[]{:S(2)}) async-start(), calls=%async_computation.6 | async-start | bytes 786432 | tf_op jit(solution)/shard_map/psum | solution.py:239
  381.7 3.4 copy-start.2
  385.1 1.9 copy-start.3
  438.6 120.4 %copy-start.1 = (bf16[256,512]{1,0:T(8,128)(2,1)S(1)}, bf16[256,512]{1,0:T(8,128)(2,1)}, u32[]{:S(2)}) copy-start(bf16[256,512]{1,0:T(8,128)(2,1)} %param.24) | copy-start | bytes 786436
Sparse Core Ops, SparseCore 0:
  41.7 31.2 reduce-scatter.6
  125.6 40.1 all-reduce.3
  183.1 51.0 all-reduce.5
  289.5 40.7 reduce-scatter.4
  332.2 22.2 all-gather.4
  356.6 25.1 all-gather.2
  438.8 34.7 all-reduce.7

commit v2 on v1

v2 whole, which is shorter than its diff:
```python
import functools

import jax
import jax.numpy as jnp
from jax import lax
from jax.experimental import pallas as pl
from jax.experimental.pallas import tpu as pltpu
from jax.sharding import PartitionSpec as P

EPS = 1e-5
ROPE_BASE = 1.0e6
TILE = 128
CHUNKS = 1
BF16 = jnp.bfloat16
F32 = jnp.float32
MESH = pl.DeviceIdType.MESH


def shard_norm(x_val, gain_vec, width_full, n, ident):
    x_f32 = x_val.astype(F32)
    rows = x_val.shape[0]
    sq_part = jnp.sum(x_f32 * x_f32, axis=-1).reshape(-1, 128)
    sq_total = jnp.sum(small_gather(sq_part, 'x', n, ident), axis=0).reshape(rows, 1)
    return (x_f32 * lax.rsqrt(sq_total / width_full + EPS) * gain_vec.astype(F32)).astype(BF16)


def rotate(vectors, positions):
    head_dim = vectors.shape[-1]
    half_dim = head_dim // 2
    inv_freq = ROPE_BASE ** (-(jnp.arange(half_dim, dtype=F32) * 2.0 / head_dim))
    angles = (positions.astype(F32)[:, None] * inv_freq[None, :])[:, None, :]
    cosine = jnp.cos(angles)
    sine_val = jnp.sin(angles)
    first_half = vectors[..., :half_dim].astype(F32)
    second_half = vectors[..., half_dim:].astype(F32)
    return jnp.concatenate([first_half * cosine - second_half * sine_val, second_half * cosine + first_half * sine_val], axis=-1).astype(BF16)


def attention(queries, new_keys, new_vals, key_cache, val_cache, lengths):
    head_dim = queries.shape[-1]
    steps = queries.shape[0]
    old = jnp.einsum('tbkh,bskh->bkts', queries, key_cache, preferred_element_type=F32) * head_dim ** -0.5
    new = jnp.sum(queries.astype(F32)[:, None] * new_keys.astype(F32)[None], axis=-1).transpose(2, 3, 0, 1) * head_dim ** -0.5
    old_mask = (jnp.arange(key_cache.shape[1])[None, :] < lengths[:, None])[:, None, None, :]
    new_mask = (jnp.arange(steps)[None, :] <= jnp.arange(steps)[:, None])[None, None]
    old = jnp.where(old_mask, old, -1.0e30)
    new = jnp.where(new_mask, new, -1.0e30)
    peak_val = jnp.maximum(jnp.max(old, axis=-1, keepdims=True), jnp.max(new, axis=-1, keepdims=True))
    w_old = jnp.where(old_mask, jnp.exp(old - peak_val), 0.0)
    w_new = jnp.where(new_mask, jnp.exp(new - peak_val), 0.0)
    total_w = jnp.sum(w_old, axis=-1, keepdims=True) + jnp.sum(w_new, axis=-1, keepdims=True)
    mixed = jnp.einsum('bkts,bskh->bkth', w_old.astype(BF16), val_cache, preferred_element_type=F32)
    vals = new_vals.astype(F32).transpose(1, 2, 0, 3)
    mixed = mixed + jnp.sum(w_new.astype(BF16).astype(F32)[..., None] * vals[:, :, None], axis=3)
    return (mixed / total_w).astype(BF16).transpose(2, 0, 1, 3)


def up_kernel(per_step, tile, off_ref, rows_ref, act_ref, lin_ref, out_ref):
    step = pl.program_id(0)

    @pl.when(step == 0)
    def _():
        out_ref[...] = jnp.zeros_like(out_ref)

    depth, width = act_ref.shape[1], act_ref.shape[2]
    row_iota = lax.broadcasted_iota(jnp.int32, (tile, depth), 0)
    last = rows_ref.shape[0] // tile - 1

    def products(j, i):
        lo, hi = off_ref[step * per_step + j], off_ref[step * per_step + j + 1]
        base = pl.multiple_of(i * tile, tile)
        rows = rows_ref[pl.ds(base, tile), :].astype(F32)
        rows = jnp.where((row_iota >= lo - base) & (row_iota < hi - base), rows, 0.0).astype(BF16)
        act = jnp.dot(rows, act_ref[j], preferred_element_type=F32).astype(BF16)
        lin = jnp.dot(rows, lin_ref[j], preferred_element_type=F32).astype(BF16)
        return base, act, lin

    def add(base, act, lin):
        out_ref[pl.ds(base, tile), :width] += act
        out_ref[pl.ds(base, tile), width:] += lin

    for j in range(0, per_step, 2):
        firsts = [jnp.minimum(off_ref[step * per_step + k] // tile, last) for k in (j, j + 1)]
        for item in [products(k, i) for k, i in zip((j, j + 1), firsts)]:
            add(*item)
        for k, i in zip((j, j + 1), firsts):

            def visit(i, carry):
                add(*products(k, i))
                return carry

            lax.fori_loop(i + 1, (off_ref[step * per_step + k + 1] + tile - 1) // tile, visit, 0)


def down_kernel(per_step, tile, off_ref, u_ref, w_ref, out_ref, acc_ref):
    step = pl.program_id(0)

    @pl.when(step == 0)
    def _():
        acc_ref[...] = jnp.zeros_like(acc_ref)

    width, depth = w_ref.shape[1], w_ref.shape[2]
    row_iota = lax.broadcasted_iota(jnp.int32, (tile, width), 0)
    last = u_ref.shape[0] // tile - 1

    def product(j, i):
        lo, hi = off_ref[step * per_step + j], off_ref[step * per_step + j + 1]
        base = pl.multiple_of(i * tile, tile)
        rows = u_ref[pl.ds(base, tile), :].astype(F32)
        rows = jnp.where((row_iota >= lo - base) & (row_iota < hi - base), rows, 0.0).astype(BF16)
        return base, jnp.dot(rows, w_ref[j], preferred_element_type=F32)

    def add(base, out):
        acc_ref[pl.ds(base, tile), :] += out

    for j in range(0, per_step, 2):
        firsts = [jnp.minimum(off_ref[step * per_step + k] // tile, last) for k in (j, j + 1)]
        for item in [product(k, i) for k, i in zip((j, j + 1), firsts)]:
            add(*item)
        for k, i in zip((j, j + 1), firsts):

            def visit(i, carry):
                add(*product(k, i))
                return carry

            lax.fori_loop(i + 1, (off_ref[step * per_step + k + 1] + tile - 1) // tile, visit, 0)

    @pl.when(step == pl.num_programs(0) - 1)
    def _():
        def cut(i, carry):
            at = pl.ds(pl.multiple_of(i * tile, tile), tile)
            rest = acc_ref[at, :]
            for k in range(3):
                term = rest.astype(BF16)
                out_ref[at, k * depth:(k + 1) * depth] = term
                rest = rest - term.astype(F32)
            return carry

        lax.fori_loop(0, acc_ref.shape[0] // tile, cut, 0)


def experts_up(offsets, rows, w_act, w_lin):
    experts, depth, width = w_act.shape
    pairs = rows.shape[0]
    per_step = 4
    return pl.pallas_call(
        functools.partial(up_kernel, per_step, TILE),
        out_shape=jax.ShapeDtypeStruct((pairs, 2 * width), BF16),
        grid_spec=pltpu.PrefetchScalarGridSpec(
            num_scalar_prefetch=1,
            grid=(experts // per_step,),
            in_specs=[
                pl.BlockSpec((pairs, depth), lambda s, off: (0, 0), pipeline_mode=pl.Buffered(1)),
                pl.BlockSpec((per_step, depth, width), lambda s, off: (s, 0, 0)),
                pl.BlockSpec((per_step, depth, width), lambda s, off: (s, 0, 0)),
            ],
            out_specs=pl.BlockSpec((pairs, 2 * width), lambda s, off: (0, 0), pipeline_mode=pl.Buffered(1)),
        ),
        compiler_params=pltpu.CompilerParams(dimension_semantics=("arbitrary",), vmem_limit_bytes=40 << 20),
        cost_estimate=pl.CostEstimate(flops=12 << 30, bytes_accessed=24 << 20, transcendentals=0),
        name="experts_up",
    )(offsets, rows, w_act, w_lin)


def experts_down(offsets, unit, w_down):
    experts, width, depth = w_down.shape
    pairs = unit.shape[0]
    per_step = 4
    return pl.pallas_call(
        functools.partial(down_kernel, per_step, TILE),
        out_shape=jax.ShapeDtypeStruct((pairs, 3 * depth), BF16),
        grid_spec=pltpu.PrefetchScalarGridSpec(
            num_scalar_prefetch=1,
            grid=(experts // per_step,),
            in_specs=[
                pl.BlockSpec(unit.shape, lambda s, off: (0, 0), pipeline_mode=pl.Buffered(1)),
                pl.BlockSpec((per_step, width, depth), lambda s, off: (s, 0, 0)),
            ],
            out_specs=pl.BlockSpec((pairs, 3 * depth), lambda s, off: (0, 0), pipeline_mode=pl.Buffered(1)),
            scratch_shapes=[pltpu.VMEM((pairs, depth), F32)],
        ),
        compiler_params=pltpu.CompilerParams(dimension_semantics=("arbitrary",), vmem_limit_bytes=48 << 20),
        cost_estimate=pl.CostEstimate(flops=12 << 30, bytes_accessed=12 << 20, transcendentals=0),
        name="experts_down",
    )(offsets, unit, w_down)


def cache_kernel(block, depth, steps, len_ref, new_ref, cache_ref, out_ref, buf, in_sem, out_sem):
    chunks = cache_ref.shape[0] // block
    slots = 2 * depth

    def read(c):
        return pltpu.make_async_copy(cache_ref.at[pl.ds(c * block, block)], buf.at[c % slots], in_sem.at[c % slots])

    def write(c):
        return pltpu.make_async_copy(buf.at[c % slots], out_ref.at[pl.ds(c * block, block)], out_sem.at[c % slots])

    for c in range(depth):
        read(c).start()

    def body(c, carry):
        @pl.when(c >= depth)
        def _():
            write(c - depth).wait()

        @pl.when(c + depth < chunks)
        def _():
            read(c + depth).start()

        read(c).wait()
        for j in range(block):
            b = c * block + j
            buf[c % slots, j, pl.ds(len_ref[b], steps)] = new_ref[b]
        write(c).start()
        return carry

    lax.fori_loop(0, chunks, body, 0)
    for k in range(depth):
        write(chunks - depth + k).wait()


def write_cache(lengths, new_rows, cache, name):
    block, depth = 8, 4
    return pl.pallas_call(
        functools.partial(cache_kernel, block, depth, new_rows.shape[1]),
        out_shape=jax.ShapeDtypeStruct(cache.shape, cache.dtype),
        in_specs=[pl.BlockSpec(memory_space=pltpu.SMEM), pl.BlockSpec(memory_space=pltpu.VMEM), pl.BlockSpec(memory_space=pltpu.HBM)],
        out_specs=pl.BlockSpec(memory_space=pltpu.HBM),
        scratch_shapes=[
            pltpu.VMEM((2 * depth, block) + cache.shape[1:], cache.dtype),
            pltpu.SemaphoreType.DMA((2 * depth,)),
            pltpu.SemaphoreType.DMA((2 * depth,)),
        ],
        compiler_params=pltpu.CompilerParams(vmem_limit_bytes=20 << 20),
        cost_estimate=pl.CostEstimate(flops=0, bytes_accessed=2 * cache.size * 2, transcendentals=0),
        name=name,
    )(lengths, new_rows, cache)


def greet(axis, peers):
    barrier = pltpu.get_barrier_semaphore()
    for peer in peers:
        pl.semaphore_signal(barrier, inc=1, device_id={axis: peer}, device_id_type=MESH)
    pl.semaphore_wait(barrier, len(peers))


def gather_kernel(axis, n, in_ref, out_ref, send_sem, recv_sem):
    me = lax.axis_index(axis)
    peers = [lax.rem(me + d, n) for d in range(1, n)]
    greet(axis, peers)
    copies = []
    for d, peer in enumerate(peers):
        copies.append(pltpu.make_async_remote_copy(src_ref=in_ref, dst_ref=out_ref.at[me], send_sem=send_sem.at[d], recv_sem=recv_sem.at[d], device_id={axis: peer}, device_id_type=MESH))
        copies[-1].start()
    out_ref[me] = in_ref[...]
    for copy in copies:
        copy.wait()


def small_gather(arr, axis, n, ident):
    return pl.pallas_call(
        functools.partial(gather_kernel, axis, n),
        out_shape=jax.ShapeDtypeStruct((n,) + arr.shape, arr.dtype),
        in_specs=[pl.BlockSpec(memory_space=pltpu.VMEM)],
        out_specs=pl.BlockSpec(memory_space=pltpu.VMEM),
        scratch_shapes=[pltpu.SemaphoreType.DMA((n - 1,)), pltpu.SemaphoreType.DMA((n - 1,))],
        compiler_params=pltpu.CompilerParams(collective_id=ident, has_side_effects=True),
        name=f"gather_{ident}",
    )(arr)


def pair_gather_kernel(axis, n, in_ref, out_ref, send_sem, recv_sem, fwd_send, fwd_recv):
    me = lax.axis_index(axis)
    partner = me + 1 - 2 * lax.rem(me, 2)
    chips = n // 2
    peers = [lax.rem(me + 2 * d, n) for d in range(1, chips)]
    greet(axis, peers + [partner])

    def copy(src, dst, send, recv, peer):
        out = pltpu.make_async_remote_copy(src_ref=src, dst_ref=dst, send_sem=send, recv_sem=recv, device_id={axis: peer}, device_id_type=MESH)
        out.start()
        return out

    first = [copy(in_ref, out_ref.at[me], send_sem.at[d], recv_sem.at[d], peer) for d, peer in enumerate(peers + [partner])]
    out_ref[me] = in_ref[...]
    second = []
    for d in range(1, chips):
        first[d - 1].wait_recv()
        origin = lax.rem(me + n - 2 * d, n)
        second.append(copy(out_ref.at[origin], out_ref.at[origin], fwd_send.at[d - 1], fwd_recv.at[d - 1], partner))
    first[-1].wait_recv()
    for item in second:
        item.wait_recv()
    for item in first + second:
        item.wait_send()


def pair_gather(arr, axis, n, ident):
    chips = n // 2
    return pl.pallas_call(
        functools.partial(pair_gather_kernel, axis, n),
        out_shape=jax.ShapeDtypeStruct((n,) + arr.shape, arr.dtype),
        in_specs=[pl.BlockSpec(memory_space=pltpu.VMEM)],
        out_specs=pl.BlockSpec(memory_space=pltpu.VMEM),
        scratch_shapes=[pltpu.SemaphoreType.DMA((chips,)), pltpu.SemaphoreType.DMA((chips,)), pltpu.SemaphoreType.DMA((chips - 1,)), pltpu.SemaphoreType.DMA((chips - 1,))],
        compiler_params=pltpu.CompilerParams(collective_id=ident, has_side_effects=True),
        name=f"pair_gather_{ident}",
    )(arr)


def sum_kernel(axis, n, in_ref, out_ref, part_ref, total_ref, send_a, recv_a, send_b, recv_b):
    me = lax.axis_index(axis)
    peers = [lax.rem(me + d, n) for d in range(1, n)]
    greet(axis, peers)
    first = []
    for d, peer in enumerate(peers):
        first.append(pltpu.make_async_remote_copy(src_ref=in_ref.at[peer], dst_ref=part_ref.at[d], send_sem=send_a.at[d], recv_sem=recv_a.at[d], device_id={axis: peer}, device_id_type=MESH))
        first[-1].start()
    for copy in first:
        copy.wait_recv()
    total = in_ref[me].astype(F32)
    for d in range(n - 1):
        total = total + part_ref[d].astype(F32)
    total_ref[...] = total.astype(total_ref.dtype)
    out_ref[me] = total_ref[...]
    second = []
    for d, peer in enumerate(peers):
        second.append(pltpu.make_async_remote_copy(src_ref=total_ref, dst_ref=out_ref.at[me], send_sem=send_b.at[d], recv_sem=recv_b.at[d], device_id={axis: peer}, device_id_type=MESH))
        second[-1].start()
    for copy in second:
        copy.wait_recv()
    for copy in first + second:
        copy.wait_send()


def small_sum(arr, axis, n, ident):
    block = (arr.shape[0] // n, arr.shape[1])
    sems = [pltpu.SemaphoreType.DMA((n - 1,))] * 4
    return pl.pallas_call(
        functools.partial(sum_kernel, axis, n),
        out_shape=jax.ShapeDtypeStruct((n,) + block, arr.dtype),
        in_specs=[pl.BlockSpec(memory_space=pltpu.VMEM)],
        out_specs=pl.BlockSpec(memory_space=pltpu.VMEM),
        scratch_shapes=[pltpu.VMEM((n - 1,) + block, arr.dtype), pltpu.VMEM(block, arr.dtype)] + sems,
        compiler_params=pltpu.CompilerParams(collective_id=ident, has_side_effects=True),
        name=f"sum_{ident}",
    )(arr.reshape((n,) + block)).reshape(arr.shape)


def scatter_kernel(axis, n, in_ref, k_ref, v_ref, out_ref, my_k_ref, my_v_ref, part_ref, acc_ref, far_ref, side_ref, near_ref, hold_ref, local_sem, store_sem, send_a, recv_a, send_b, recv_b):
    me = lax.axis_index(axis)
    core = lax.rem(me, 2)
    partner = me + 1 - 2 * core
    chips = n // 2
    turn = 4 * core - 2
    after = lax.rem(me + turn + n, n)
    ahead = lax.rem(me - turn + n, n)
    across = lax.rem(me + 2 * (chips // 2), n)
    greet(axis, [partner, after, ahead])

    def copy(src, dst, send, recv, peer):
        out = pltpu.make_async_remote_copy(src_ref=src, dst_ref=dst, send_sem=send, recv_sem=recv, device_id={axis: peer}, device_id_type=MESH)
        out.start()
        return out

    order = [across, ahead, after, me]
    first = []
    for d, place in enumerate([across, after, ahead, me]):
        first.append(copy(in_ref.at[place + partner - me], part_ref.at[d], send_a.at[d], recv_a.at[d], partner))
    part = my_k_ref.shape[0]
    reads = []
    for d, src in enumerate((k_ref, v_ref)):
        reads.append(pltpu.make_async_copy(src.at[pl.ds(me * part, part)], hold_ref.at[d], local_sem.at[d]))
        reads[-1].start()

    def pair_sum(d):
        first[d].wait_recv()
        return in_ref[order[d]].astype(F32) + part_ref[d].astype(F32)

    acc_ref[0] = pair_sum(0).astype(acc_ref.dtype)
    far = copy(acc_ref.at[0], far_ref, send_b.at[0], recv_b.at[0], after)
    acc_ref[1] = pair_sum(1).astype(acc_ref.dtype)
    side = copy(acc_ref.at[1], side_ref, send_b.at[1], recv_b.at[1], ahead)
    mid = pair_sum(2)
    far.wait_recv()
    acc_ref[2] = (mid + far_ref[...].astype(F32)).astype(acc_ref.dtype)
    near = copy(acc_ref.at[2], near_ref, send_b.at[2], recv_b.at[2], after)
    stores = []
    for d, dst in enumerate((my_k_ref, my_v_ref)):
        reads[d].wait()
        stores.append(pltpu.make_async_copy(hold_ref.at[d], dst, store_sem.at[d]))
        stores[-1].start()
    own = pair_sum(3)
    side.wait_recv()
    own = own + side_ref[...].astype(F32)
    near.wait_recv()
    out_ref[...] = (own + near_ref[...].astype(F32)).astype(out_ref.dtype)
    for item in first + [far, side, near]:
        item.wait_send()
    for item in stores:
        item.wait()


def scatter_rows(arr, k_cache, v_cache, axis, n, ident):
    rows, cols = arr.shape
    block = (rows // n, cols)
    mine = (k_cache.shape[0] // n,) + k_cache.shape[1:]
    vmem = pl.BlockSpec(memory_space=pltpu.VMEM)
    return pl.pallas_call(
        functools.partial(scatter_kernel, axis, n),
        out_shape=(jax.ShapeDtypeStruct(block, arr.dtype), jax.ShapeDtypeStruct(mine, k_cache.dtype), jax.ShapeDtypeStruct(mine, v_cache.dtype)),
        in_specs=[vmem, pl.BlockSpec(memory_space=pl.ANY), pl.BlockSpec(memory_space=pl.ANY)],
        out_specs=(vmem, pl.BlockSpec(memory_space=pltpu.HBM), pl.BlockSpec(memory_space=pltpu.HBM)),
        scratch_shapes=[pltpu.VMEM((4,) + block, arr.dtype), pltpu.VMEM((3,) + block, arr.dtype)] + [pltpu.VMEM(block, arr.dtype)] * 3
        + [pltpu.VMEM((2,) + mine, k_cache.dtype), pltpu.SemaphoreType.DMA((2,)), pltpu.SemaphoreType.DMA((2,)), pltpu.SemaphoreType.DMA((4,)), pltpu.SemaphoreType.DMA((4,)), pltpu.SemaphoreType.DMA((3,)), pltpu.SemaphoreType.DMA((3,))],
        compiler_params=pltpu.CompilerParams(collective_id=ident, has_side_effects=True, vmem_limit_bytes=40 << 20),
        name=f"scatter_{ident}",
    )(arr.reshape((n,) + block), k_cache, v_cache)


def solution(mesh):
    nx, ny = mesh.shape['x'], mesh.shape['y']
    cache_spec = P('dp', None, 'y', None)
    in_specs = (P(None, 'dp'), P('dp'), P(None, 'dp', None), P(None, 'x'), cache_spec, cache_spec, P('x'), P('x', 'y'), P('x', 'y'), P('x', 'y'), P('y', 'x'), P('x'), P('x', None), P(None, 'x', 'y'), P(None, 'x', 'y'), P(None, 'y', 'x'))
    out_specs = (P(None, 'dp', 'x'), cache_spec, cache_spec)

    def per_device(tokens, lengths, choices, emb_table, k_cache, v_cache, g_attn, w_q, w_k, w_v, w_o, g_ffn, w_router, w_act, w_lin, w_down):
        steps, batch = tokens.shape
        top = choices.shape[2]
        heads, head_dim = k_cache.shape[2], k_cache.shape[3]
        cols = heads * head_dim
        width_full = emb_table.shape[1] * nx
        experts = w_act.shape[0]
        my_x = lax.axis_index('x')
        part = batch // nx
        rows = steps * batch
        pairs = rows * top

        def to_rows(arr):
            return arr.reshape((steps, nx, part) + arr.shape[2:]).swapaxes(0, 1).reshape((rows,) + arr.shape[2:])

        def from_rows(arr):
            return arr.reshape((nx, steps, part) + arr.shape[1:]).swapaxes(0, 1).reshape((steps, batch) + arr.shape[1:])

        choice_rows = to_rows(choices)
        member = jnp.any(choice_rows[:, :, None] == jnp.arange(experts)[None, None, :], axis=1)
        member_f = member.astype(F32)
        before = (jnp.arange(rows)[None, :] < jnp.arange(rows)[:, None]).astype(BF16)
        rank = jnp.dot(before, member.astype(BF16), preferred_element_type=F32)
        counts = jnp.sum(member_f, axis=0)
        ends = jnp.cumsum(counts)
        starts = ends - counts
        place = (rank + starts[None, :]).astype(jnp.int32)
        offsets = jnp.concatenate([starts, ends[-1:]]).astype(jnp.int32)
        high = jnp.where(member, place // 128, 255).astype(BF16)
        low = jnp.where(member, place % 128, 0).astype(BF16)
        places = jnp.arange(pairs).astype(F32)
        pair_expert = (places[:, None] >= starts[None, :]) & (places[:, None] < ends[None, :])
        left = jnp.concatenate([jnp.where(pair_expert, 128.0, 0.0), jnp.where(pair_expert, 1.0, 0.0)], axis=1).astype(BF16)
        right = jnp.concatenate([high, low], axis=1)
        pick = (lax.dot_general(left, right, (((1,), (1,)), ((), ())), preferred_element_type=F32) == places[:, None]).astype(BF16)
        put = (lax.dot_general(right, left, (((1,), (1,)), ((), ())), preferred_element_type=F32) == places[None, :]).astype(BF16)
        put = lax.optimization_barrier(put)
        chunk = pairs // CHUNKS
        share = chunk // nx

        x_in = jnp.take(emb_table, to_rows(tokens), axis=0)
        normed = shard_norm(x_in, g_attn, width_full, nx, 0)
        w_qkv = jnp.concatenate([w_q, w_k, w_v], axis=1)
        proj_part = jnp.dot(normed, w_qkv, preferred_element_type=F32).astype(BF16)
        proj, my_keys, my_vals = scatter_rows(proj_part, k_cache, v_cache, 'x', nx, 6)
        my_lengths = lax.dynamic_slice_in_dim(lengths, my_x * part, part)
        my_positions = my_lengths[None, :] + jnp.arange(steps)[:, None]
        flat_positions = my_positions.reshape(-1)
        queries = rotate(proj[:, :cols].reshape(-1, heads, head_dim), flat_positions)
        new_keys = rotate(proj[:, cols:2 * cols].reshape(-1, heads, head_dim), flat_positions)
        new_vals = proj[:, 2 * cols:].reshape(-1, heads, head_dim)

        def split(arr):
            return arr.reshape(steps, part, heads, head_dim)

        mixed = attention(split(queries), split(new_keys), split(new_vals), my_keys, my_vals, my_lengths).reshape(-1, cols)
        mixed_all = pair_gather(mixed, 'x', nx, 2).reshape(rows, cols)

        new_kv = jnp.concatenate([new_keys.reshape(-1, cols), proj[:, 2 * cols:]], axis=1)
        kv_all = lax.all_gather(new_kv, 'x', axis=0, tiled=True)
        kv_all = kv_all.reshape(nx, steps, part, 2, heads, head_dim).transpose(3, 0, 2, 1, 4, 5).reshape(2, batch, steps, heads, head_dim)
        attn_part = jnp.dot(mixed_all, w_o, preferred_element_type=F32).astype(BF16)
        attn_sum = small_sum(attn_part, 'y', ny, 3)
        x_mid = (x_in.astype(F32) + attn_sum.astype(F32)).astype(BF16)
        normed2 = shard_norm(x_mid, g_ffn, width_full, nx, 1)
        normed2, new_k, new_v = lax.optimization_barrier((normed2, kv_all[0], kv_all[1]))
        k_out = write_cache(lengths, new_k, k_cache, "write_keys")
        v_out = write_cache(lengths, new_v, v_cache, "write_vals")
        logits = small_sum(jnp.dot(normed2, w_router, preferred_element_type=F32), 'x', nx, 4)
        masked = jnp.where(member, logits, -jnp.inf)
        expd = jnp.exp(masked - jnp.max(masked, axis=1, keepdims=True))
        coef = expd / jnp.sum(expd, axis=1, keepdims=True)
        width = w_act.shape[2]

        def bounds(c):
            return jnp.clip(offsets - c * chunk, 0, chunk)

        hidden = []
        for c in range(CHUNKS):
            pair_rows = jnp.dot(pick[c * chunk:(c + 1) * chunk], normed2, preferred_element_type=F32).astype(BF16)
            hidden_part = experts_up(bounds(c), pair_rows, w_act, w_lin)
            hidden.append(lax.psum_scatter(hidden_part, 'x', scatter_dimension=0, tiled=True))
        unit_all = []
        for c in range(CHUNKS):
            own_expert = lax.dynamic_slice_in_dim(pair_expert, c * chunk + my_x * share, share).astype(F32)
            own_token = lax.dynamic_slice_in_dim(pick, c * chunk + my_x * share, share).astype(F32)
            own_gate = jnp.sum(own_expert * jnp.dot(own_token, coef, precision=lax.Precision.HIGHEST, preferred_element_type=F32), axis=1, keepdims=True)
            if c == CHUNKS - 1:
                own_gate, k_out = lax.optimization_barrier((own_gate, k_out))
            act, lin = hidden[c][:, :width].astype(F32), hidden[c][:, width:].astype(F32)
            unit_all.append(lax.all_gather((own_gate * jax.nn.silu(act) * lin).astype(BF16), 'x', axis=0, tiled=True))
        terms = 0.0
        for c in range(CHUNKS):
            if c == CHUNKS - 1:
                unit_all[c], v_out = lax.optimization_barrier((unit_all[c], v_out))
            terms = terms + jnp.dot(put[:, c * chunk:(c + 1) * chunk], experts_down(bounds(c), unit_all[c], w_down), preferred_element_type=F32)
        depth = w_down.shape[2]
        moe_part = (terms[:, :depth] + terms[:, depth:2 * depth] + terms[:, 2 * depth:]).astype(BF16)
        moe_sum = small_sum(moe_part, 'y', ny, 5)
        hidden_out = (x_mid.astype(F32) + moe_sum.astype(F32)).astype(BF16)
        return from_rows(hidden_out), k_out, v_out

    return jax.shard_map(per_device, mesh=mesh, in_specs=in_specs, out_specs=out_specs, check_vma=False)
```

time: 566 us -> 305 us (0.54)
  waiting for transfers between devices: 205 us -> 0.2 us
  other arithmetic: 147 us -> 18 us
  Pallas kernels: 102 us -> 175 us
  blocking collectives: 49.6 us -> 0 us
  local copies, waits for them, and re-layouts: 30.2 us -> 56.6 us
  matrix products: 15.1 us -> 39.7 us
    select_n x2 -> x0, other arithmetic: 137 us -> none  [write_slots(): cache_arr = jnp.where(hit_mask, new_rows[step_idx][:, None], cache_arr)]
    pallas_call x0 -> x9, Pallas kernels: none -> 129 us  [the longest x3 55.2 us: small_sum(): pl.pallas_call(functools.partial(sum_kernel, axis, n), out_shape=jax.Shap...]
    psum x3 -> x0, waiting for transfers between devices: 90.8 us -> none  [the longest x1 50.9 us: per_device(): lax.psum(jnp.dot(normed2, w_router, preferred_element_type=F32), 'x')]
    reduce_scatter x2 -> x1, waiting for transfers between devices: 67.5 us -> 0.02 us  [per_device(): lax.psum_scatter(hidden_part, 'x', scatter_dimension=0, tiled=True)]
    all_gather x2, waiting for transfers between devices: 46.8 us -> 0.02 us  [the longest x1 0.02 us: per_device(): lax.all_gather((own_gate * jax.nn.silu(act) * lin).astype(BF16), 'x', axi...]
    pallas_call x1, Pallas kernels: 50.9 us -> 21.7 us  [experts_up(): pl.pallas_call(functools.partial(up_kernel, per_step, TILE), out_shape=ja...]
    psum x2 -> x0, blocking collectives: 28.5 us -> none  [shard_norm(): sq_total = lax.psum(jnp.sum(x_f32 * x_f32, axis=-1, keepdims=True), 'x')]
    dot_general x6 -> x8, matrix products: 7.72 us -> 35.9 us  [the longest x1 10.1 us: per_device(): jnp.dot(put[:, c * chunk:(c + 1) * chunk], experts_down(bounds(c), unit_a...]
  transfers between devices with their start and end apart: 7 -> 3, of which waited for: 6 -> 0; matrix products, arithmetic and copies ran while one was open for 23% -> 13% of each run, Pallas kernels for 0% -> 29%
where the time goes in v2:
time: 305 us; the launch traced here: 304 us
  Pallas kernels  175 us (57%)
  local copies, waits for them, and re-layouts  56.6 us (19%)
  matrix products  39.7 us (13%)
  other arithmetic  18 us (6%)
  between operations  14.3 us (5%)
    pallas_call x3, Pallas kernels, small_sum(): pl.pallas_call(functools.partial(sum_kernel, axis, n), out_shape=jax.Shap...  55.2 us
    unnamed x37, local copies, waits for them, and re-layouts  32.3 us
    pallas_call x1, Pallas kernels, experts_down(): pl.pallas_call(functools.partial(down_kernel, per_step, TILE), out_shape=...  24.3 us
    pallas_call x2, Pallas kernels, write_cache(): pl.pallas_call(functools.partial(cache_kernel, block, depth, new_rows.sha...  24.1 us
    pallas_call x1, Pallas kernels, experts_up(): pl.pallas_call(functools.partial(up_kernel, per_step, TILE), out_shape=ja...  21.7 us
    pallas_call x2, Pallas kernels, small_gather(): pl.pallas_call(functools.partial(gather_kernel, axis, n), out_shape=jax.S...  17 us
    pallas_call x1, Pallas kernels, scatter_rows(): pl.pallas_call(functools.partial(scatter_kernel, axis, n), out_shape=(jax...  16.6 us
    pallas_call x1, Pallas kernels, pair_gather(): pl.pallas_call(functools.partial(pair_gather_kernel, axis, n), out_shape=...  16.1 us
  transfers between devices with their start and end apart: 3, of which 0 were waited for; matrix products, arithmetic and copies ran while one was open for 13% of the time, Pallas kernels for 29%

profile of v2, /device:TPU:97, one launch (start us, length us, event | category | flops | bytes accessed | tf_op | source)
XLA Modules:
  0.0 304.3 jit_solution(7279693349105408351)
XLA Ops:
  7.3 0.8 reshape.360
  8.3 13.7 %gather_fusion = bf16[768,256]{1,0:T(8,128)(2,1)S(1)} fusion(bf16[50304,256]{1,0:T(8,128)(2,1)} %param.19, s32[1024]{0:T(1024)S(1)} %pad_clamp_fusion), kind=kCustom, calls=%fused_computation | custom fusion | bytes 789504 | tf_op jit(solution)/shard_map/jit(_take)/gather | solution.py:467
  22.0 0.9 fusion.39
  22.9 8.7 %gather_0.1 = f32[8,6,128]{2,1,0:T(8,128)} custom-call(f32[6,128]{1,0:T(8,128)} %bitcast.116), custom_call_target="tpu_custom_call" | custom-call | tf_op jit(solution)/shard_map/gather_0/pallas_call | solution.py:261
  31.7 0.8 reduce_sum.100
  32.4 0.7 convert_element_type.201
  33.1 1.9 convolution_convert_fusion.1
  35.1 16.6 %scatter_6.1 = (bf16[96,1536]{1,0:T(8,128)(2,1)S(1)}, bf16[32,128,4,128]{3,2,1,0:T(4,128)(2,1)S(1)}, bf16[32,128,4,128]{3,2,1,0:T(4,128)(2,1)S(1)}) custom-call(bf16[8,96,1536]{2,1,0:T(8,128)(2,1)S(1)} %bitcast.89, bf16[256,128,4,128]{3,2,1,0:T(4,128)(2,1)} %cache_ref.2, bf16[256,128,4,128]{3,2,1,0:T(4,128)(2,1)} %cache_ref.3), custom_call_target="tpu_custom_call" | custom-call | tf_op jit(solution)/shard_map/scatter_6/pallas_call | solution.py:409
  51.7 2.0 copy-done.6
  53.7 2.0 copy-done.7
  56.0 0.2 fusion.97
  56.2 0.2 multiply_cosine_fusion
  56.4 0.1 fusion.60
  56.7 0.7 pad_maximum_fusion.4
  57.4 0.2 reduce-scatter.2.cloned.1.call-start
  58.0 4.6 %fusion.99 = (f32[32,4,3]{2,1,0:T(4,128)S(1)}, f32[32,4,3,128]{3,2,1,0:T(4,128)S(1)}) fusion(bf16[32,128,4,128]{3,2,1,0:T(4,128)(2,1)} %copy-done.7, bf16[3,32,4,128]{3,1,0,2:T(8,128)(2,1)S(1)} %pad_maximum_fusion.7, pred[32,128]{1,0:T(8,128)(4,1)S(1)} %iota_compare_fusion.7), kind=kOutput, calls=%fused_computation.161 | convolution fusion | flops 12729984 | bytes 4494848 | tf_op jit(solution)/shard_map/tbkh,bskh->bkts/dot_general | solution.py:42
  62.6 0.3 multiply_reduce_fusion.2
  63.6 0.4 fusion.73
  64.1 0.2 multiply_reduce_fusion.1
  64.3 3.5 %fusion.31 = bf16[3,32,4,128]{3,0,2,1:T(4,128)(2,1)S(1)} fusion(bf16[32,128,4,128]{3,2,1,0:T(4,128)(2,1)} %copy-done.6, f32[32,4,3,128]{3,0,2,1:T(8,128)S(1)} %multiply_reduce_fusion.1, f32[32,4,3,128]{3,2,1,0:T(4,128)S(1)} %get-tuple-element.48, f32[3,32,4]{0,2,1:T(4,128)S(1)} %add_bitcast_fusion, f32[32,4,3]{2,1,0:T(4,128)S(1)} %copy.120, ...), kind=kOutput, calls=%fused_computation.33 | convolution fusion | flops 12877824 | bytes 4692992 | tf_op jit(solution)/shard_map/bkts,bskh->bkth/dot_general | solution.py:52
  67.9 0.7 copy.187
  68.5 16.1 %pair_gather_2.1 = bf16[8,96,512]{2,1,0:T(8,128)(2,1)} custom-call(bf16[96,512]{1,0:T(8,128)(2,1)} %bitcast.112), custom_call_target="tpu_custom_call" | custom-call | tf_op jit(solution)/shard_map/pair_gather_2/pallas_call | solution.py:300
  84.7 2.2 convolution_convert_fusion.2
  86.9 17.1 %sum_3.1 = bf16[4,192,256]{2,1,0:T(8,128)(2,1)} custom-call(bf16[4,192,256]{2,1,0:T(8,128)(2,1)} %bitcast.98), custom_call_target="tpu_custom_call" | custom-call | tf_op jit(solution)/shard_map/sum_3/pallas_call | solution.py:339
  104.1 1.4 multiply_reduce_fusion
  105.5 0.7 reshape.374.in_ref
  106.2 8.3 %gather_1.1 = f32[8,6,128]{2,1,0:T(8,128)} custom-call(f32[6,128]{1,0:T(8,128)} %reshape.374.in_ref), custom_call_target="tpu_custom_call" | custom-call | tf_op jit(solution)/shard_map/gather_1/pallas_call | solution.py:261
  114.5 0.8 reduce_sum.107
  115.5 0.2 fusion.7
  116.1 0.5 slice.73
  116.7 0.5 fusion.64
  117.2 0.7 fusion.88.off_ref
  118.0 1.0 multiply_convert_fusion
  119.0 0.3 select_convert_fusion.1
  119.4 0.9 copy-done.11
  120.2 4.6 %convolution_compare_fusion = pred[6144,768]{1,0:T(32,128)(4,1)} fusion(f32[6144]{0:T(1024)S(1)} %iota_convert_fusion, bf16[6144,64]{0,1:T(8,128)(2,1)S(1)} %get-tuple-element.42, bf16[6144,64]{0,1:T(8,128)(2,1)S(1)} %get-tuple-element.41, bf16[768,64]{0,1:T(8,128)(2,1)S(1)} %get-tuple-element.34, bf16[768,64]{0,1:T(8,128)(2,1)S(1)} %get-tuple-element.33), kind=kOutput, calls=%fused_computation.2 | convolution fusion | flops 1216217088 | bytes 6512640 | tf_op jit(solution)/shard_map/dot_general | solution.py:461
  124.8 2.8 reshape.375
  127.7 0.7 copy.185
  128.4 0.6 fusion.95
  129.0 1.0 copy-done.17
  130.0 3.8 %convolution_convert_fusion.rows_ref = bf16[6144,256]{1,0:T(8,128)(2,1)S(1)} fusion(pred[6144,768]{1,0:T(32,128)(4,1)S(1)} %copy-done.17, bf16[768,256]{1,0:T(8,128)(2,1)} %multiply_convert_fusion), kind=kOutput, calls=%fused_computation.3 | convolution fusion | flops 2417491968 | bytes 8257536 | tf_op jit(solution)/shard_map/dot_general | solution.py:506
  133.9 21.7 %experts_up.1 = bf16[6144,512]{1,0:T(8,128)(2,1)S(1)} custom-call(s32[65]{0:T(128)S(1)} %fusion.88.off_ref, bf16[6144,256]{1,0:T(8,128)(2,1)S(1)} %convolution_convert_fusion.rows_ref, bf16[64,256,256]{2,1,0:T(8,128)(2,1)} %act_ref.1, bf16[64,256,256]{2,1,0:T(8,128)(2,1)} %lin_ref.1), custom_call_target="tpu_custom_call" | custom-call | flops 12884901888 | bytes 25165824 | tf_op jit(solution)/shard_map/experts_up/pallas_call | solution.py:146
  155.6 2.7 copy-done.4
  158.4 0.2 copy.133
  158.6 1.1 compare_and_fusion
  159.8 10.5 %copy-done.2 = bf16[256,128,4,128]{3,2,1,0:T(4,128)(2,1)S(1)} copy-done((bf16[256,128,4,128]{3,2,1,0:T(4,128)(2,1)S(1)}, bf16[256,128,4,128]{3,2,1,0:T(4,128)(2,1)}, u32[]{:S(2)}) %copy-start.2) | copy-done | bytes 33554456
  170.3 12.2 %write_keys.1 = bf16[256,128,4,128]{3,2,1,0:T(4,128)(2,1)} custom-call(s32[256]{0:T(256)S(1)} %copy-done.5, bf16[256,3,4,128]{3,2,1,0:T(4,128)(2,1)S(1)} %bitcast.88, bf16[256,128,4,128]{3,2,1,0:T(4,128)(2,1)S(1)} %copy-done.2), custom_call_target="tpu_custom_call" | custom-call | bytes 67108864 | tf_op jit(solution)/shard_map/write_keys/pallas_call | solution.py:224
  182.6 1.0 fusion.100
  183.5 21.8 %sum_4.1 = f32[8,96,64]{2,1,0:T(8,128)} custom-call(f32[8,96,64]{2,1,0:T(8,128)} %bitcast.96), custom_call_target="tpu_custom_call" | custom-call | tf_op jit(solution)/shard_map/sum_4/pallas_call | solution.py:339
  205.4 1.2 fusion.70
  206.7 1.4 exponential_reduce_fusion
  208.1 1.8 copy.132
  209.9 2.3 fusion.25
  212.3 2.2 fusion.50
  214.6 5.1 %compare_convert_fusion = bf16[768,6144]{1,0:T(8,128)(2,1)} fusion(f32[6144]{0:T(1024)S(1)} %iota_convert_fusion, bf16[6144,64]{0,1:T(8,128)(2,1)S(1)} %copy-done.12, bf16[6144,64]{0,1:T(8,128)(2,1)S(1)} %get-tuple-element.41, bf16[768,64]{0,1:T(8,128)(2,1)S(1)} %get-tuple-element.34, bf16[768,64]{0,1:T(8,128)(2,1)S(1)} %get-tuple-element.33), kind=kOutput, calls=%fused_computation.1 | convolution fusion | flops 1220935680 | bytes 11231232 | tf_op jit(solution)/shard_map/dot_general | solution.py:462
  219.7 10.5 %copy-done.3 = bf16[256,128,4,128]{3,2,1,0:T(4,128)(2,1)S(1)} copy-done((bf16[256,128,4,128]{3,2,1,0:T(4,128)(2,1)S(1)}, bf16[256,128,4,128]{3,2,1,0:T(4,128)(2,1)}, u32[]{:S(2)}) %copy-start.3) | copy-done | bytes 33554456
  230.3 11.9 %write_vals.1 = bf16[256,128,4,128]{3,2,1,0:T(4,128)(2,1)} custom-call(s32[256]{0:T(256)S(1)} %copy-done.5, bf16[256,3,4,128]{3,2,1,0:T(4,128)(2,1)S(1)} %bitcast.87, bf16[256,128,4,128]{3,2,1,0:T(4,128)(2,1)S(1)} %copy-done.3), custom_call_target="tpu_custom_call" | custom-call | bytes 67108864 | tf_op jit(solution)/shard_map/write_vals/pallas_call | solution.py:224
  242.2 1.9 copy-done.8
  244.1 24.3 %experts_down.1 = bf16[6144,768]{1,0:T(8,128)(2,1)} custom-call(s32[65]{0:T(128)S(1)} %fusion.88.off_ref, bf16[6144,256]{1,0:T(8,128)(2,1)S(1)} %copy-done.8, bf16[64,256,256]{2,1,0:T(8,128)(2,1)} %w_ref.1), custom_call_target="tpu_custom_call" | custom-call | flops 12884901888 | bytes 12582912 | tf_op jit(solution)/shard_map/experts_down/pallas_call | solution.py:169
  268.5 10.1 %fusion.101 = f32[768,768]{1,0:T(8,128)S(1)} fusion(bf16[768,6144]{1,0:T(8,128)(2,1)S(1)} %copy-done.9, bf16[6144,768]{1,0:T(8,128)(2,1)} %experts_down.1), kind=kOutput, calls=%fused_computation.163 | convolution fusion | flops 7247757312 | bytes 21233664 | tf_op jit(solution)/shard_map/dot_general | solution.py:522
  278.6 0.9 fusion.43
  279.5 16.2 %sum_5.1 = bf16[4,192,256]{2,1,0:T(8,128)(2,1)} custom-call(bf16[4,192,256]{2,1,0:T(8,128)(2,1)} %bitcast.99), custom_call_target="tpu_custom_call" | custom-call | tf_op jit(solution)/shard_map/sum_5/pallas_call | solution.py:339
  295.7 1.3 fusion.51
  297.0 0.8 copy.134
  (84 shorter events, 2.9 us)
Async XLA Ops:
  7.2 77.5 %copy-start = (bf16[512,256]{1,0:T(8,128)(2,1)S(1)}, bf16[512,256]{1,0:T(8,128)(2,1)}, u32[]{:S(2)}) copy-start(bf16[512,256]{1,0:T(8,128)(2,1)} %param.26) | copy-start | bytes 786436
  7.2 117.6 %all-gather.3.cloned.1.call-start = ((), (), s32[]{:S(2)}) async-start(), calls=%async_computation.1 | async-start | bytes 1769472 | tf_op jit(solution)/shard_map/all_gather | solution.py:486
  35.0 20.7 %copy-start.5 = (s32[256]{0:T(256)S(1)}, s32[256]{0:T(256)}, u32[]{:S(2)}) copy-start(s32[256]{0:T(256)} %len_ref.3) | copy-start | bytes 3076
  51.7 2.0 copy-start.6
  53.7 2.0 copy-start.7
  57.4 154.9 %reduce-scatter.2.cloned.1.call-start = ((), (), s32[]{:S(2)}) async-start(), calls=%async_computation.2 | async-start | bytes 7077888 | tf_op jit(solution)/shard_map/reduce_scatter | solution.py:508
  64.3 50.9 %copy-start.15 = (s32[3,256,8]{1,2,0:T(8,128)S(1)}, s32[3,256,8]{1,2,0:T(8,128)}, u32[]{:S(2)}) copy-start(s32[3,256,8]{1,2,0:T(8,128)} %param.18) | copy-start | bytes 73732
  67.8 50.1 %copy-start.16 = (bf16[256]{0:T(256)(128)(2,1)S(1)}, bf16[256]{0:T(256)(128)(2,1)}, u32[]{:S(2)}) copy-start(bf16[256]{0:T(256)(128)(2,1)} %param.27) | copy-start | bytes 1540
  104.0 13.9 %copy-start.10 = (bf16[4,192,256]{2,1,0:T(8,128)(2,1)S(1)}, bf16[4,192,256]{2,1,0:T(8,128)(2,1)}, u32[]{:S(2)}) copy-start(bf16[4,192,256]{2,1,0:T(8,128)(2,1)} %sum_3.1) | copy-start | bytes 1179652
  119.3 0.9 copy-start.11
  127.7 2.3 copy-start.17
  155.5 2.7 copy-start.4
  158.3 83.9 %all-gather.5.cloned.1.call-start = ((), (), s32[]{:S(2)}) async-start(), calls=%async_computation.3 | async-start | bytes 3538944 | tf_op jit(solution)/shard_map/all_gather | solution.py:517
  159.8 10.5 %copy-start.2 = (bf16[256,128,4,128]{3,2,1,0:T(4,128)(2,1)S(1)}, bf16[256,128,4,128]{3,2,1,0:T(4,128)(2,1)}, u32[]{:S(2)}) copy-start(bf16[256,128,4,128]{3,2,1,0:T(4,128)(2,1)} %cache_ref.2) | copy-start | bytes 100663296
  170.3 12.2 %copy-start.13 = (bf16[768,256]{1,0:T(8,128)(2,1)S(1)}, bf16[768,256]{1,0:T(8,128)(2,1)}, u32[]{:S(2)}) copy-start(bf16[768,256]{1,0:T(8,128)(2,1)} %multiply_convert_fusion) | copy-start | bytes 1179652
  170.3 12.2 %copy-start.14 = (bf16[256,64]{0,1:T(8,128)(2,1)S(1)}, bf16[256,64]{0,1:T(8,128)(2,1)}, u32[]{:S(2)}) copy-start(bf16[256,64]{0,1:T(8,128)(2,1)} %param.28) | copy-start | bytes 98308
  182.5 32.0 %copy-start.12 = (bf16[6144,64]{0,1:T(8,128)(2,1)S(1)}, bf16[6144,64]{0,1:T(8,128)(2,1)}, u32[]{:S(2)}) copy-start(bf16[6144,64]{0,1:T(8,128)(2,1)} %copy-done.11) | copy-start | bytes 2359300
  219.7 10.5 %copy-start.3 = (bf16[256,128,4,128]{3,2,1,0:T(4,128)(2,1)S(1)}, bf16[256,128,4,128]{3,2,1,0:T(4,128)(2,1)}, u32[]{:S(2)}) copy-start(bf16[256,128,4,128]{3,2,1,0:T(4,128)(2,1)} %cache_ref.3) | copy-start | bytes 100663296
  242.2 1.9 copy-start.8
  244.1 24.3 %copy-start.9 = (bf16[768,6144]{1,0:T(8,128)(2,1)S(1)}, bf16[768,6144]{1,0:T(8,128)(2,1)}, u32[]{:S(2)}) copy-start(bf16[768,6144]{1,0:T(8,128)(2,1)} %compare_convert_fusion) | copy-start | bytes 28311556
  268.5 29.3 %copy-start.1 = (bf16[512,256]{1,0:T(8,128)(2,1)S(1)}, bf16[512,256]{1,0:T(8,128)(2,1)}, u32[]{:S(2)}) copy-start(bf16[512,256]{1,0:T(8,128)(2,1)} %param.26) | copy-start | bytes 786436
Sparse Core Ops, SparseCore 0:
  57.6 27.3 all-gather.2
  158.4 46.4 reduce-scatter.1
  214.7 22.6 all-gather.4
